TPU v7x, 128 devices: a whole 4x4x4 slice. The times are simulated.
128 devices in a mesh: tok: 64 (over x, y, z), col: 2 (over core).
Axes of the slice: x: 4, y: 4, z: 4, core: 2. Of those that a mesh axis runs over, the one named last changes fastest.
Arguments:
- first_acts: bfloat16 [98304, 4096], P('tok', 'col'), as said below
- second_acts: bfloat16 [98304, 4096], P('tok', 'col'), as said below
- window_counts: int32 [256], P('tok'), may hold values from 96 to 384, as said below
Outputs:
- whitened: float32 [4096, 4096], P('tok', 'col')
- means: float32 [2, 4096], P(None, 'col')
Inputs may be any that keep to these rules, and one draw needn't show every extreme that they name: `window_counts`: the live tokens of a window are its first ones; on every index of tok one of its 4 windows is full with 384 live tokens. `first_acts`: real values of order one to some tens; slots that are not live hold values too. `second_acts`: real values of order one to some tens; slots that are not live hold values too.
All inputs are finite; a program needn't handle non-finite values.
Results may differ from a plain program's by a relative error of at most 0.0003.
Values may be sent and summed in bfloat16 or wider, within the bound.
A program may use at most 192 MiB of HBM per device.

v0:
```python
import functools

import jax
import jax.numpy as jnp
from jax import lax
from jax.sharding import Mesh
from jax.sharding import PartitionSpec as P

TOK = ("tok_0", "tok_1", "tok_2")


contract_rows = (((0,), (0,)), ((), ()))


def from_everyone(x, axis):
    size = lax.axis_size(axis)
    return lax.all_to_all(jnp.broadcast_to(x[None], (size, *x.shape)), axis, 0, 0, tiled=True)


def in_order(parts, dim):
    lengths = list(parts.shape[1:])
    lengths[dim] *= parts.shape[0]
    return jnp.moveaxis(parts, 0, dim).reshape(lengths)


def collect(x, axis, dim):
    parts = from_everyone(x, axis)
    return in_order(parts, dim)


def one_axis_at_a_time(x, axes):
    return functools.reduce(lax.psum, axes, x)


def sent_together(arrays, axis, dim, along):
    columns = [a.reshape(*a.shape[:along], -1) for a in arrays]
    both = jnp.concatenate(columns, axis=along)
    result, at, finished = (lax.all_gather(both, axis, axis=dim, tiled=True), 0, [])
    for a, column in zip(arrays, columns):
        slab = result[..., at : at + column.shape[along]]
        finished.append(slab.reshape(*slab.shape[:along], *a.shape[along:]))
        at += column.shape[along]
    return tuple(finished)


def local(first_acts, second_acts, window_counts):
    windows = window_counts.shape[0]
    slot_count = first_acts.shape[0] // windows
    half_width = first_acts.shape[1]
    col_index = lax.axis_index("col")
    full_width = half_width * lax.axis_size("col")
    row_width = full_width // lax.axis_size(TOK)
    row_offset = lax.axis_index(TOK) * row_width
    count_float = window_counts.astype(jnp.float32)
    live_mask = lax.broadcasted_iota(jnp.int32, (windows, slot_count), 1) < window_counts[:, None]
    mask_half = live_mask.astype(jnp.bfloat16)
    first_win = first_acts.reshape(windows, slot_count, half_width)
    second_win = second_acts.reshape(windows, slot_count, half_width)
    mean_first_part = (
        jnp.einsum("ws,wsd->wd", mask_half, first_win, preferred_element_type=jnp.float32)
        / count_float[:, None]
    )
    mean_second = (
        jnp.einsum("ws,wsd->wd", mask_half, second_win, preferred_element_type=jnp.float32)
        / count_float[:, None]
    )
    centered_first = jnp.where(
        live_mask[:, :, None], first_win - mean_first_part[:, None, :], 0.0
    ).astype(jnp.bfloat16)
    centered_first = centered_first.reshape(windows * slot_count, half_width)
    centered_second = jnp.where(
        live_mask[:, :, None], second_win - mean_second[:, None, :], 0.0
    ).astype(jnp.bfloat16)
    centered_second = centered_second.reshape(windows * slot_count, half_width)
    whole_first = lax.all_gather(centered_first, "col", axis=1, tiled=True)
    window_mean_first = collect(mean_first_part, "col", 1)
    square_first = jnp.sum(jnp.square(whole_first.astype(jnp.float32)), axis=0)
    square_second = jnp.sum(jnp.square(centered_second.astype(jnp.float32)), axis=0)
    device_count = jnp.sum(count_float)
    sum_first = jnp.sum(count_float[:, None] * window_mean_first, axis=0)
    sum_second = jnp.sum(count_float[:, None] * mean_second, axis=0)
    device_first = sum_first / device_count
    device_second = sum_second / device_count
    shift_first = window_mean_first - device_first[None, :]
    shift_second = mean_second - device_second[None, :]
    part_first = square_first + jnp.sum(count_float[:, None] * jnp.square(shift_first), axis=0)
    part_second = square_second + jnp.sum(count_float[:, None] * jnp.square(shift_second), axis=0)
    spread_first, spread_second = (
        one_axis_at_a_time(part_first, TOK),
        one_axis_at_a_time(part_second, TOK),
    )
    peer_count, peer_first, peer_second = sent_together(
        (device_count.reshape(1), device_first[None, :], device_second[None, :]), TOK, 0, 1
    )
    grand_count = jnp.sum(peer_count)
    grand_first = jnp.sum(peer_count[:, None] * peer_first, axis=0) / grand_count
    grand_second = jnp.sum(peer_count[:, None] * peer_second, axis=0) / grand_count
    peer_shift_first = peer_first - grand_first[None, :]
    peer_shift_second = peer_second - grand_second[None, :]
    spread_first = spread_first + jnp.sum(
        peer_count[:, None] * jnp.square(peer_shift_first), axis=0
    )
    spread_second = spread_second + jnp.sum(
        peer_count[:, None] * jnp.square(peer_shift_second), axis=0
    )
    late_left = lax.dynamic_slice_in_dim(
        peer_count[:, None] * peer_shift_first, row_offset, row_width, 1
    )
    early_left = count_float[:, None] * shift_first
    product = lax.dot_general(
        whole_first, centered_second, contract_rows, preferred_element_type=jnp.float32
    )
    cross = lax.psum_scatter(
        product
        + lax.dot_general(
            early_left,
            shift_second,
            contract_rows,
            precision=lax.Precision.HIGHEST,
            preferred_element_type=jnp.float32,
        ),
        TOK,
        scatter_dimension=0,
        tiled=True,
    )
    cross = cross + lax.dot_general(
        late_left,
        peer_shift_second,
        contract_rows,
        precision=lax.Precision.HIGHEST,
        preferred_element_type=jnp.float32,
    )
    var_first = lax.dynamic_slice_in_dim(spread_first, row_offset, row_width) / grand_count
    var_second = spread_second / grand_count
    whitened = (
        cross / grand_count / jnp.sqrt((var_first[:, None] + 0.1) * (var_second[None, :] + 0.1))
    )
    means = jnp.stack(
        [lax.dynamic_slice_in_dim(grand_first, col_index * half_width, half_width), grand_second]
    )
    return (whitened, means)


def solution(mesh):
    torus = Mesh(
        mesh.devices.reshape(4, 4, 4, mesh.shape["col"]), ("tok_0", "tok_1", "tok_2", "col")
    )
    return jax.shard_map(
        local,
        mesh=torus,
        in_specs=(P(TOK, "col"), P(TOK, "col"), P(TOK)),
        out_specs=(P(TOK, "col"), P(None, "col")),
        check_vma=False,
    )
```

profile of v0, /device:TPU:0, one launch (start us, length us, event | category | flops | bytes accessed | tf_op | source)
XLA Modules:
  0.0 566.9 jit_solution(5087924848903745424)
XLA Ops:
  7.2 0.0 all-gather.4.cloned.1.call-start
  7.2 1.3 convert_reduce_fusion
  8.5 0.7 convert_element_type.27
  9.1 0.7 iota_compare_fusion
  9.9 0.0 copy-start.1
  9.9 0.0 copy-start
  9.9 3.9 fusion.17
  13.7 0.7 copy-done.1
  14.5 0.9 fusion.19
  15.4 0.1 multiply_reduce_fusion.7
  15.5 0.7 broadcast_divide_fusion.3
  16.2 0.1 multiply_reduce_fusion.6
  16.3 0.0 copy-done
  16.3 6.4 %multiply_reduce_fusion.1 = (f32[2048]{0:T(1024)S(1)}, bf16[1536,2048]{1,0:T(8,128)(2,1)}, bf16[1536,2048]{1,0:T(8,128)(2,1)}) fusion(f32[4,2048]{1,0:T(4,128)S(1)} %get-tuple-element.15, bf16[1536,2048]{1,0:T(8,128)(2,1)S(1)} %copy-done, pred[1536]{0:T(1024)(128)(4,1)S(1)} %lt.24, f32[4,2048]{1,0:T(4,128)S(1)} %get-tuple-element.18, ...), kind=kLoop, calls=%fused_computation.8 | loop fusion | flops 34600960 | bytes 25241088 | tf_op jit(solution)/shard_map/reduce_sum | solution.py:78
  22.7 0.0 all-gather.4.cloned.1.call-update
  22.8 0.0 all-gather.6.cloned.1.call-start
  22.8 3.8 all_to_all.5
  26.6 0.1 fusion.10
  26.7 0.7 fusion.32
  27.4 1.4 concatenate.3
  28.8 0.0 all-gather.6.cloned.1.call-update
  28.9 0.0 reduce-scatter.2.cloned.1.call-start
  28.9 0.7 fusion.33
  29.6 30.4 %fusion.11 = f32[4096,2048]{1,0:T(8,128)} fusion(f32[4,4096]{1,0:T(4,128)S(1)} %bitcast.64, f32[4096]{0:T(1024)S(1)} %bitcast.65, f32[4]{0:T(128)S(1)} %convert_element_type.27, f32[4,2048]{1,0:T(4,128)S(1)} %get-tuple-element.15, f32[2048]{0:T(1024)S(1)} %broadcast_divide_fusion.3), kind=kOutput, calls=%fused_computation.26 | convolution fusion | flops 402694144 | bytes 33677328 | tf_op jit(solution)/shard_map/dot_general | solution.py:115
  60.0 0.0 all-gather.4.cloned.1.call-done
  60.0 37.9 %convolution_add_fusion = f32[4096,2048]{1,0:T(8,128)} fusion(f32[4096,2048]{1,0:T(8,128)} %fusion.11, bf16[1536,4096]{1,0:T(8,128)(2,1)} %all-gather.4.cloned.1.call-done, bf16[1536,2048]{1,0:T(8,128)(2,1)} %get-tuple-element.13), kind=kOutput, calls=%fused_computation.1 | convolution fusion | flops 25778192384 | bytes 85983232 | tf_op jit(solution)/shard_map/dot_general | solution.py:110
  97.9 0.0 reduce-scatter.2.cloned.1.call-update
  97.9 0.7 broadcast_divide_fusion.1
  98.6 0.1 fusion.9
  98.7 23.8 %all-gather.6.cloned.1.call-done = f32[64,1,6145]{2,1,0:T(1,128)} async-done(((f32[1,1,6145]{2,1,0:T(1,128)}), f32[64,1,6145]{2,1,0:T(1,128)}) %all-gather.6.cloned.1.call-update) | async-done | bytes 1573136 | tf_op jit(solution)/shard_map/all_gather | solution.py:38
  122.5 1.5 copy.20
  124.0 0.7 slice_reduce_fusion
  124.7 0.4 multiply_reduce_fusion.3
  125.1 0.7 broadcast_divide_fusion
  125.8 0.2 multiply_reduce_fusion.5
  126.0 0.7 broadcast_divide_fusion.2
  126.7 0.2 multiply_reduce_fusion.4
  126.9 0.6 pad_maximum_fusion
  127.6 0.4 multiply_reduce_fusion.2
  127.9 7.5 %multiply_reduce_fusion = f32[4096]{0:T(1024)S(1)} fusion(bf16[1536,4096]{1,0:T(8,128)(2,1)} %all-gather.4.cloned.1.call-done), kind=kLoop, calls=%fused_computation | loop fusion | flops 18870272 | bytes 12599296 | tf_op jit(solution)/shard_map/reduce_sum | solution.py:77
  135.4 14.8 %all-reduce.2 = (f32[2048]{0:T(1024)S(1)}, f32[4096]{0:T(1024)S(1)}) all-reduce(f32[2048]{0:T(1024)S(1)} %add.68, f32[4096]{0:T(1024)S(1)} %add.64), channel_id=1, replica_groups=mesh['tok_0'=4,'tok_1'=4,'tok_2'=4,'col'=2] {'tok_0'}, use_global_device_ids=true, to_apply=%region_15.16 | all-reduce | flops 6144 | bytes 49152 | tf_op jit(solution)/shard_map/psum | solution.py:32
  150.3 21.6 %all-reduce.1 = (f32[2048]{0:T(1024)S(1)}, f32[4096]{0:T(1024)S(1)}) all-reduce(f32[2048]{0:T(1024)S(1)} %get-tuple-element.8, f32[4096]{0:T(1024)S(1)} %get-tuple-element.9), channel_id=1, replica_groups=mesh['tok_0'=4,'tok_1'=4,'tok_2'=4,'col'=2] {'tok_1'}, use_global_device_ids=true, to_apply=%region_16.17 | all-reduce | flops 6144 | bytes 49152 | tf_op jit(solution)/shard_map/psum | solution.py:32
  171.9 43.5 %all-reduce = (f32[2048]{0:T(1024)S(1)}, f32[4096]{0:T(1024)S(1)}) all-reduce(f32[2048]{0:T(1024)S(1)} %get-tuple-element.6, f32[4096]{0:T(1024)S(1)} %get-tuple-element.7), channel_id=1, replica_groups=mesh['tok_0'=4,'tok_1'=4,'tok_2'=4,'col'=2] {'tok_2'}, use_global_device_ids=true, to_apply=%region_17.18 | all-reduce | flops 6144 | bytes 49152 | tf_op jit(solution)/shard_map/psum | solution.py:32
  215.4 0.8 fusion.24
  216.2 0.7 divide_add_fusion
  216.9 340.1 %reduce-scatter.2.cloned.1.call-done = f32[64,2048]{1,0:T(8,128)} async-done(((f32[4096,2048]{1,0:T(8,128)}), f32[64,2048]{1,0:T(8,128)}) %reduce-scatter.2.cloned.1.call-update) | async-done | bytes 524304 | tf_op jit(solution)/shard_map/reduce_scatter | solution.py:113
  557.0 3.4 fusion.5
  (8 shorter events, 0.1 us)
Async XLA Ops:
  7.2 52.8 %all-gather.4.cloned.1.call-start = ((), (), s32[]{:S(2)}) async-start(), calls=%async_computation.2 | async-start | bytes 18874368 | tf_op jit(solution)/shard_map/all_gather | solution.py:75
  9.9 4.6 copy-start.1
  9.9 6.4 %copy-start = (bf16[1536,2048]{1,0:T(8,128)(2,1)S(1)}, bf16[1536,2048]{1,0:T(8,128)(2,1)}, u32[]{:S(2)}) copy-start(bf16[1536,2048]{1,0:T(8,128)(2,1)} %param.4) | copy-start | bytes 18874372
  22.8 99.7 %all-gather.6.cloned.1.call-start = ((), (), s32[]{:S(2)}) async-start(), calls=%async_computation.4 | async-start | bytes 1630720 | tf_op jit(solution)/shard_map/all_gather | solution.py:38
  28.9 528.1 %reduce-scatter.2.cloned.1.call-start = ((), (), s32[]{:S(2)}) async-start(), calls=%async_computation.3 | async-start | bytes 34078720 | tf_op jit(solution)/shard_map/reduce_scatter | solution.py:113
Sparse Core Ops, SparseCore 0:
  22.9 29.8 all-gather.3
  56.2 66.2 all-gather.5
  124.9 432.0 reduce-scatter.1
where the time goes:
time: 567 us
  waiting for transfers between devices  364 us (64%)
  blocking collectives  83.8 us (15%)
  matrix products  76.4 us (13%)
  other arithmetic  25 us (4%)
  between operations  13.9 us (2%)
    reduce_scatter x1, waiting for transfers between devices, local(): lax.psum_scatter(product + lax.dot_general(early_left, shift_second, cont...  340 us
    psum x3, blocking collectives, one_axis_at_a_time(): return functools.reduce(lax.psum, axes, x)  80 us
    dot_general x1, matrix products, local(): lax.dot_general(whole_first, centered_second, contract_rows, preferred_el...  37.9 us
    dot_general x1, matrix products, local(): lax.dot_general(early_left, shift_second, contract_rows, precision=lax.Pr...  30.4 us
    all_gather x1, waiting for transfers between devices, sent_together(): lax.all_gather(both, axis, axis=dim, tiled=True)  23.8 us
  transfers between devices with their start and end apart: 3, of which 2 were waited for; matrix products, arithmetic and copies ran while one was open for 15% of the time, Pallas kernels for 0%

commit v1 on v0

v1 whole, which is shorter than its diff:
```python
import functools

import jax
import jax.numpy as jnp
from jax import lax
from jax.experimental import pallas as pl
from jax.experimental.pallas import tpu as pltpu
from jax.sharding import Mesh
from jax.sharding import PartitionSpec as P

TOK = ("tok_0", "tok_1", "tok_2")
MESH = pl.DeviceIdType.MESH
STRIDE = (16, 4, 1)
LANE = 128
AUX = 128
CODES = 32767.0
contract_rows = (((0,), (0,)), ((), ()))


def center_kernel(
    counts_ref, first_ref, second_ref, left_ref, right_ref, left_aux, right_aux, stats_ref, means, squares
):
    window = pl.program_id(0)
    windows = pl.num_programs(0)
    slots, width = first_ref.shape
    live_count = counts_ref[window]
    count_float = live_count.astype(jnp.float32)
    live = lax.broadcasted_iota(jnp.int32, (slots, LANE), 0) < live_count
    eight = lax.broadcasted_iota(jnp.int32, (8, LANE), 0)

    @pl.when(window == 0)
    def _():
        squares[...] = jnp.zeros_like(squares)
        means[...] = jnp.zeros_like(means)

    def centered_of(ref, which, cs):
        x = jnp.where(live, ref[:, cs].astype(jnp.float32), 0.0)
        mean = jnp.sum(x, axis=0, keepdims=True) / count_float
        means[which, :, cs] = jnp.where(eight == window, mean, means[which, :, cs])
        centered = jnp.where(live, x - mean, 0.0).astype(jnp.bfloat16)
        wide = centered.astype(jnp.float32)
        squares[which : which + 1, cs] += jnp.sum(wide * wide, axis=0, keepdims=True)
        return centered

    def chunk(j, _):
        cs = pl.ds(pl.multiple_of(j * LANE, LANE), LANE)
        left_ref[cs, :] = centered_of(first_ref, 0, cs).T
        right_ref[:, cs] = centered_of(second_ref, 1, cs)
        return 0

    lax.fori_loop(0, width // LANE, chunk, 0)

    @pl.when(window == windows - 1)
    def _():
        counts = [counts_ref[w].astype(jnp.float32) for w in range(4)]
        total = counts[0] + counts[1] + counts[2] + counts[3]
        row = lax.broadcasted_iota(jnp.int32, (16, LANE), 0)

        def rows_of(which, cs, weighted):
            mean = [means[which, w : w + 1, cs] for w in range(4)]
            device = sum(counts[w] * mean[w] for w in range(4)) / total
            shift = [m - device for m in mean]
            part = squares[which : which + 1, cs] + sum(counts[w] * shift[w] * shift[w] for w in range(4))
            stats_ref[which : which + 1, cs] = device
            stats_ref[which + 2 : which + 3, cs] = part
            packed = jnp.zeros((16, LANE), jnp.float32)
            for w in range(4):
                value = counts[w] * shift[w] if weighted else shift[w]
                high = value.astype(jnp.bfloat16).astype(jnp.float32)
                low = value - high
                order = (high, high, low, low) if weighted else (high, low, high, low)
                for k in range(4):
                    packed = jnp.where(row == 4 * k + w, order[k], packed)
            return jnp.concatenate([packed, jnp.zeros((AUX - 16, LANE), jnp.float32)], axis=0)

        def tail(j, _):
            cs = pl.ds(pl.multiple_of(j * LANE, LANE), LANE)
            left_aux[cs, :] = rows_of(0, cs, True).T.astype(jnp.bfloat16)
            right_aux[:, cs] = rows_of(1, cs, False).astype(jnp.bfloat16)
            return 0

        lax.fori_loop(0, width // LANE, tail, 0)


def center(first_acts, second_acts, window_counts):
    windows = window_counts.shape[0]
    tokens, width = first_acts.shape
    slots = tokens // windows
    bf16 = jnp.bfloat16
    return pl.pallas_call(
        center_kernel,
        grid=(windows,),
        in_specs=[
            pl.BlockSpec(memory_space=pltpu.SMEM),
            pl.BlockSpec((slots, width), lambda w: (w, 0)),
            pl.BlockSpec((slots, width), lambda w: (w, 0)),
        ],
        out_specs=[
            pl.BlockSpec((width, slots), lambda w: (0, w)),
            pl.BlockSpec((slots, width), lambda w: (w, 0)),
            pl.BlockSpec((width, AUX), lambda w: (0, 0)),
            pl.BlockSpec((AUX, width), lambda w: (0, 0)),
            pl.BlockSpec((8, width), lambda w: (0, 0)),
        ],
        out_shape=[
            jax.ShapeDtypeStruct((width, tokens), bf16),
            jax.ShapeDtypeStruct((tokens, width), bf16),
            jax.ShapeDtypeStruct((width, AUX), bf16),
            jax.ShapeDtypeStruct((AUX, width), bf16),
            jax.ShapeDtypeStruct((8, width), jnp.float32),
        ],
        scratch_shapes=[pltpu.VMEM((2, 8, width), jnp.float32), pltpu.VMEM((8, width), jnp.float32)],
        compiler_params=pltpu.CompilerParams(
            dimension_semantics=("arbitrary",), vmem_limit_bytes=48 * 1024 * 1024
        ),
        cost_estimate=pl.CostEstimate(flops=40_000_000, bytes_accessed=28_000_000, transcendentals=0),
        name="center",
    )(window_counts, first_acts, second_acts)


DIMS = ((0, 1, 2), (1, 2, 0), (2, 0, 1))


def widths_of(width):
    tiles = width // LANE
    cut = [tiles // 3 + (1 if q < tiles % 3 else 0) for q in range(3)]
    return [c * LANE for c in cut]


def product_kernel(
    widths,
    left_hbm, right_hbm, left_aux_hbm, right_aux_hbm, out_ref,
    left, right, sums, send1, recv1, sscale1, rscale1, send2, recv2, sscale2, rscale2,
    send3, recv3, sscale3, rscale3,
    local_sem, peer_send, peer_recv, s1, r1, t1, u1, s2, r2, t2, u2, s3, r3, t3, u3,
):
    me = [lax.axis_index(name) for name in TOK]
    core = lax.axis_index("col")
    tokens = left_hbm.shape[2]
    half_blocks = left.shape[0] // 2
    starts = [sum(widths[:q]) for q in range(3)]

    barrier = pltpu.get_barrier_semaphore()
    for d in range(3):
        for step in (1, 3):
            pl.semaphore_signal(
                barrier, inc=1, device_id={TOK[d]: lax.rem(me[d] + step, 4)}, device_id_type=MESH
            )
    pl.semaphore_signal(barrier, inc=1, device_id={"col": 1 - core}, device_id_type=MESH)

    mine = pl.ds(core * half_blocks, half_blocks)
    local = [
        pltpu.make_async_copy(left_hbm, left.at[mine, :, pl.ds(0, tokens)], local_sem.at[0]),
        pltpu.make_async_copy(left_aux_hbm, left.at[mine, :, pl.ds(tokens, AUX)], local_sem.at[1]),
        pltpu.make_async_copy(right_hbm, right.at[pl.ds(0, tokens)], local_sem.at[2]),
        pltpu.make_async_copy(right_aux_hbm, right.at[pl.ds(tokens, AUX)], local_sem.at[3]),
    ]
    for copy in local:
        copy.start()
    pl.semaphore_wait(barrier, 7)
    peer = [
        pltpu.make_async_remote_copy(
            left_hbm, left.at[mine, :, pl.ds(0, tokens)], peer_send.at[0], peer_recv.at[0],
            device_id={"col": 1 - core}, device_id_type=MESH,
        ),
        pltpu.make_async_remote_copy(
            left_aux_hbm, left.at[mine, :, pl.ds(tokens, AUX)], peer_send.at[1], peer_recv.at[1],
            device_id={"col": 1 - core}, device_id_type=MESH,
        ),
    ]
    for copy in peer:
        copy.start()
    for copy in local:
        copy.wait()
    for copy in peer:
        copy.wait()

    def columns(q):
        return pl.ds(starts[q], widths[q])

    def tile(q, j):
        return pl.ds(pl.multiple_of(starts[q] + j * LANE, LANE), LANE)

    def multiply(q, to_a, to_b):
        a, b, g = DIMS[q]
        blocks = []
        for distance in (2, 1, 3, 0):
            to_g = lax.rem(me[g] + distance, 4)
            blocks.append(left[to_a * STRIDE[a] + to_b * STRIDE[b] + to_g * STRIDE[g]])
        sums[:, columns(q)] = jnp.dot(
            jnp.concatenate(blocks, axis=0), right[:, columns(q)], preferred_element_type=jnp.float32
        )

    def encoded(p, code_ref, scale_ref):
        peak = jnp.maximum(jnp.max(jnp.abs(p), axis=0, keepdims=True), 1e-30)
        code = jnp.round(p * (CODES / peak)).astype(jnp.int32)
        code_ref[...] = code.astype(jnp.int16)
        scale_ref[...] = peak * (1.0 / CODES)

    def decoded(code_ref, scale_ref):
        return code_ref[...].astype(jnp.int32).astype(jnp.float32) * scale_ref[...]

    def each_tile(q, body):
        def step(j, _):
            body(tile(q, j))
            return 0

        lax.fori_loop(0, widths[q] // LANE, step, 0)

    def copies1(q, slot, target):
        to = {TOK[DIMS[q][0]]: target}
        cs = columns(q)
        return (
            pltpu.make_async_remote_copy(
                send1.at[slot, :, cs], recv1.at[slot, :, cs], s1.at[q, slot], r1.at[q, slot],
                device_id=to, device_id_type=MESH,
            ),
            pltpu.make_async_remote_copy(
                sscale1.at[slot, :, cs], rscale1.at[slot, :, cs], t1.at[q, slot], u1.at[q, slot],
                device_id=to, device_id_type=MESH,
            ),
        )

    def start(copies):
        for copy in copies:
            copy.start()

    def arrived(copies):
        for copy in copies:
            copy.wait_recv()

    def left_of(copies):
        for copy in copies:
            copy.wait_send()

    def towards(q, i):
        return lax.rem(me[DIMS[q][0]] + 1 + 2 * lax.rem(i, 2), 4)

    def early_far(i, _):
        for q in range(3):
            a, b, g = DIMS[q]
            distance = jnp.where(i < 2, 2 + i, 3 - i)
            multiply(q, lax.rem(me[a] + 2, 4), lax.rem(me[b] + distance, 4))

            def body(cs):
                encoded(sums[:, cs], send1.at[i, :, cs], sscale1.at[i, :, cs])

            each_tile(q, body)
            start(copies1(q, i, towards(q, i)))
        return 0

    def near_plain(i, _):
        for q in range(3):
            a, b, g = DIMS[q]
            distance = jnp.where(i < 2, 3 - i, i - 2)
            multiply(q, towards(q, i), lax.rem(me[b] + distance, 4))

            def body(cs):
                encoded(sums[:, cs], send1.at[4 + i, :, cs], sscale1.at[4 + i, :, cs])

            each_tile(q, body)
            start(copies1(q, 4 + i, towards(q, i)))
        return 0

    def near_adding(i, _):
        for q in range(3):
            a, b, g = DIMS[q]
            distance = jnp.where(i < 2, 2 + i, 3 - i)
            multiply(q, towards(q, i), lax.rem(me[b] + distance, 4))
            arrived(copies1(q, i, towards(q, i)))

            def body(cs):
                p = sums[:, cs] + decoded(recv1.at[i, :, cs], rscale1.at[i, :, cs])
                encoded(p, send1.at[8 + i, :, cs], sscale1.at[8 + i, :, cs])

            each_tile(q, body)
            start(copies1(q, 8 + i, towards(q, i)))
        return 0

    lax.fori_loop(0, 4, early_far, 0)
    lax.fori_loop(0, 4, near_plain, 0)
    lax.fori_loop(0, 4, near_adding, 0)

    rows = sums.shape[0]
    top, bottom = pl.ds(0, rows // 2), pl.ds(rows // 2, rows // 2)

    def copies2(q, slot, part, target):
        to = {TOK[DIMS[q][1]]: target}
        cs = columns(q)
        lines = (top, bottom)[part] if slot == 0 else pl.ds(0, rows)
        k = part if slot == 0 else slot + 1
        return (
            pltpu.make_async_remote_copy(
                send2.at[slot, lines, cs], recv2.at[slot, lines, cs], s2.at[q, k], r2.at[q, k],
                device_id=to, device_id_type=MESH,
            ),
            pltpu.make_async_remote_copy(
                sscale2.at[slot, :, cs], rscale2.at[k, :, cs], t2.at[q, k], u2.at[q, k],
                device_id=to, device_id_type=MESH,
            ),
        )

    def merged1(i, cs):
        low = jnp.where(i < 2, 8 + 2 * i, 2 * i)
        high = 5 + 2 * i
        return (
            sums[:, cs]
            + decoded(recv1.at[low, :, cs], rscale1.at[low, :, cs])
            + decoded(recv1.at[high, :, cs], rscale1.at[high, :, cs])
        )

    def own(i, _):
        for q in range(3):
            a, b, g = DIMS[q]
            after, before = lax.rem(me[b] + 1, 4), lax.rem(me[b] + 3, 4)
            distance = jnp.where(i == 0, 2, jnp.where(i == 1, 1, jnp.where(i == 2, 3, 0)))
            multiply(q, me[a], lax.rem(me[b] + distance, 4))
            arrived(copies1(q, jnp.where(i < 2, 8 + 2 * i, 2 * i), me[a]))
            arrived(copies1(q, 5 + 2 * i, me[a]))

            @pl.when(i == 0)
            def _():
                def body(cs):
                    encoded(merged1(i, cs), send2.at[0, :, cs], sscale2.at[0, :, cs])

                each_tile(q, body)
                start(copies2(q, 0, 0, after))
                start(copies2(q, 0, 1, before))

            @pl.when(i == 1)
            def _():
                arrived(copies2(q, 0, 0, after))

                def body(cs):
                    p = merged1(i, cs)
                    p = jnp.concatenate(
                        [p[: rows // 2] + decoded(recv2.at[0, top, cs], rscale2.at[0, :, cs]), p[rows // 2 :]], axis=0
                    )
                    encoded(p, send2.at[1, :, cs], sscale2.at[1, :, cs])

                each_tile(q, body)
                start(copies2(q, 1, 0, after))

            @pl.when(i == 2)
            def _():
                arrived(copies2(q, 0, 1, before))

                def body(cs):
                    p = merged1(i, cs)
                    p = jnp.concatenate(
                        [p[: rows // 2], p[rows // 2 :] + decoded(recv2.at[0, bottom, cs], rscale2.at[1, :, cs])], axis=0
                    )
                    encoded(p, send2.at[2, :, cs], sscale2.at[2, :, cs])

                each_tile(q, body)
                start(copies2(q, 2, 0, before))

            @pl.when(i == 3)
            def _():
                def body(cs):
                    sums[:, cs] = merged1(i, cs)

                each_tile(q, body)

        return 0

    lax.fori_loop(0, 4, own, 0)

    part_rows = rows // 4
    half = part_rows // 2
    first_half, second_half = pl.ds(0, half), pl.ds(half, half)

    def copies3(q, slot, part, target):
        to = {TOK[DIMS[q][2]]: target}
        cs = columns(q)
        lines = (first_half, second_half)[part] if slot == 0 else pl.ds(0, part_rows)
        k = part if slot == 0 else slot + 1
        return (
            pltpu.make_async_remote_copy(
                send3.at[slot, lines, cs], recv3.at[slot, lines, cs], s3.at[q, k], r3.at[q, k],
                device_id=to, device_id_type=MESH,
            ),
            pltpu.make_async_remote_copy(
                sscale3.at[slot, :, cs], rscale3.at[k, :, cs], t3.at[q, k], u3.at[q, k],
                device_id=to, device_id_type=MESH,
            ),
        )

    def after3(q):
        return lax.rem(me[DIMS[q][2]] + 1, 4)

    def before3(q):
        return lax.rem(me[DIMS[q][2]] + 3, 4)

    for q in range(3):
        arrived(copies2(q, 1, 0, me[DIMS[q][1]]))
        arrived(copies2(q, 2, 0, me[DIMS[q][1]]))

        def body(cs):
            p = (
                sums[:, cs]
                + decoded(recv2.at[1, :, cs], rscale2.at[2, :, cs])
                + decoded(recv2.at[2, :, cs], rscale2.at[3, :, cs])
            )
            encoded(p[:part_rows], send3.at[0, :, cs], sscale3.at[0, :, cs])
            sums[pl.ds(part_rows, 3 * part_rows), cs] = p[part_rows:]

        each_tile(q, body)
        start(copies3(q, 0, 0, after3(q)))
        start(copies3(q, 0, 1, before3(q)))

    for q in range(3):
        arrived(copies3(q, 0, 0, after3(q)))
        arrived(copies3(q, 0, 1, before3(q)))

        def body(cs):
            ahead = jnp.concatenate(
                [
                    sums[pl.ds(part_rows, half), cs] + decoded(recv3.at[0, first_half, cs], rscale3.at[0, :, cs]),
                    sums[pl.ds(part_rows + half, half), cs],
                ],
                axis=0,
            )
            encoded(ahead, send3.at[1, :, cs], sscale3.at[1, :, cs])
            behind = jnp.concatenate(
                [
                    sums[pl.ds(2 * part_rows, half), cs],
                    sums[pl.ds(2 * part_rows + half, half), cs]
                    + decoded(recv3.at[0, second_half, cs], rscale3.at[1, :, cs]),
                ],
                axis=0,
            )
            encoded(behind, send3.at[2, :, cs], sscale3.at[2, :, cs])

        each_tile(q, body)
        start(copies3(q, 1, 0, after3(q)))
        start(copies3(q, 2, 0, before3(q)))

    for q in range(3):
        arrived(copies3(q, 1, 0, after3(q)))
        arrived(copies3(q, 2, 0, before3(q)))

        def body(cs):
            out_ref[:, cs] = (
                sums[pl.ds(3 * part_rows, part_rows), cs]
                + decoded(recv3.at[1, :, cs], rscale3.at[2, :, cs])
                + decoded(recv3.at[2, :, cs], rscale3.at[3, :, cs])
            )

        each_tile(q, body)

    def drain(i, _):
        for q in range(3):
            left_of(copies1(q, i, towards(q, i)))
        return 0

    lax.fori_loop(0, 12, drain, 0)
    for q in range(3):
        for copies, towards_next, towards_last in (
            (copies2, lax.rem(me[DIMS[q][1]] + 1, 4), lax.rem(me[DIMS[q][1]] + 3, 4)),
            (copies3, after3(q), before3(q)),
        ):
            left_of(copies(q, 0, 0, towards_next))
            left_of(copies(q, 0, 1, towards_last))
            left_of(copies(q, 1, 0, towards_next))
            left_of(copies(q, 2, 0, towards_last))


def product(left, right, left_aux, right_aux):
    half_width, tokens = left.shape
    width = right.shape[1]
    block = 2 * half_width // 64
    blocks = half_width // block
    left = left.reshape(blocks, block, tokens)
    left_aux = left_aux.reshape(blocks, block, AUX)
    rows = 4 * block
    depth = tokens + AUX
    i16, f32 = jnp.int16, jnp.float32
    dma = pltpu.SemaphoreType.DMA
    return pl.pallas_call(
        functools.partial(product_kernel, widths_of(width)),
        out_shape=jax.ShapeDtypeStruct((block, width), f32),
        in_specs=[pl.BlockSpec(memory_space=pl.ANY)] * 4,
        out_specs=pl.BlockSpec(memory_space=pltpu.VMEM),
        scratch_shapes=[
            pltpu.VMEM((2 * blocks, block, depth), jnp.bfloat16),
            pltpu.VMEM((depth, width), jnp.bfloat16),
            pltpu.VMEM((rows, width), f32),
            pltpu.VMEM((12, rows, width), i16),
            pltpu.VMEM((12, rows, width), i16),
            pltpu.VMEM((12, 1, width), f32),
            pltpu.VMEM((12, 1, width), f32),
            pltpu.VMEM((3, rows, width), i16),
            pltpu.VMEM((3, rows, width), i16),
            pltpu.VMEM((3, 1, width), f32),
            pltpu.VMEM((4, 1, width), f32),
            pltpu.VMEM((3, block, width), i16),
            pltpu.VMEM((3, block, width), i16),
            pltpu.VMEM((3, 1, width), f32),
            pltpu.VMEM((4, 1, width), f32),
            dma((4,)), dma((2,)), dma((2,)),
            dma((3, 12)), dma((3, 12)), dma((3, 12)), dma((3, 12)),
            dma((3, 4)), dma((3, 4)), dma((3, 4)), dma((3, 4)),
            dma((3, 4)), dma((3, 4)), dma((3, 4)), dma((3, 4)),
        ],
        compiler_params=pltpu.CompilerParams(
            collective_id=0, has_side_effects=True, vmem_limit_bytes=67_000_000
        ),
        cost_estimate=pl.CostEstimate(
            flops=4 * half_width * width * depth, bytes_accessed=30_000_000, transcendentals=0
        ),
        name="product",
    )(left, right, left_aux, right_aux)


def local(first_acts, second_acts, window_counts):
    half_width = first_acts.shape[1]
    col_index = lax.axis_index("col")
    full_width = half_width * lax.axis_size("col")
    row_width = full_width // lax.axis_size(TOK)
    row_offset = lax.axis_index(TOK) * row_width
    left, right, left_aux, right_aux, stats = center(first_acts, second_acts, window_counts)
    device_count = jnp.sum(window_counts.astype(jnp.float32))
    first_stats = lax.all_gather(stats[0:3:2], "col", axis=1, tiled=True)
    row = jnp.concatenate(
        [first_stats[0], stats[1], first_stats[1], stats[3], device_count.reshape(1)]
    )
    peers = lax.all_gather(row[None], TOK, axis=0, tiled=True)
    cross = product(left, right, left_aux, right_aux)
    peer_count = peers[:, -1]
    f, h = full_width, half_width
    grand_count = jnp.sum(peer_count)
    peer_mean = peers[:, : f + h]
    peer_part = peers[:, f + h : 2 * (f + h)]
    grand = jnp.sum(peer_count[:, None] * peer_mean, axis=0) / grand_count
    shift = peer_mean - grand[None, :]
    var = (jnp.sum(peer_part, axis=0) + jnp.sum(peer_count[:, None] * jnp.square(shift), axis=0)) / grand_count
    late_left = lax.dynamic_slice_in_dim(shift, row_offset, row_width, 1) * peer_count[:, None]
    cross = cross + lax.dot_general(
        late_left,
        shift[:, f:],
        contract_rows,
        precision=lax.Precision.HIGHEST,
        preferred_element_type=jnp.float32,
    )
    var_first = lax.dynamic_slice_in_dim(var, row_offset, row_width)
    var_second = var[f:]
    whitened = cross / grand_count / jnp.sqrt((var_first[:, None] + 0.1) * (var_second[None, :] + 0.1))
    means = jnp.stack([lax.dynamic_slice_in_dim(grand, col_index * half_width, half_width), grand[f:]])
    return (whitened, means)


def solution(mesh):
    torus = Mesh(
        mesh.devices.reshape(4, 4, 4, mesh.shape["col"]), ("tok_0", "tok_1", "tok_2", "col")
    )
    return jax.shard_map(
        local,
        mesh=torus,
        in_specs=(P(TOK, "col"), P(TOK, "col"), P(TOK)),
        out_specs=(P(TOK, "col"), P(None, "col")),
        check_vma=False,
    )
```

time: 567 us -> 195 us (0.34)
  waiting for transfers between devices: 364 us -> 32 us
  Pallas kernels: 0 us -> 130 us
  blocking collectives: 83.8 us -> 1.82 us
  matrix products: 76.4 us -> 2.26 us
  other arithmetic: 25 us -> 4 us
  local copies, waits for them, and re-layouts: 3.77 us -> 10 us
    reduce_scatter x1 -> x0, waiting for transfers between devices: 340 us -> none  [local(): lax.psum_scatter(product + lax.dot_general(early_left, shift_second, cont...]
    pallas_call x0 -> x2, Pallas kernels: none -> 130 us  [the longest x1 110 us: product(): pl.pallas_call(functools.partial(product_kernel, widths_of(width)), out_s...]
    psum x3 -> x0, blocking collectives: 80 us -> none  [one_axis_at_a_time(): return functools.reduce(lax.psum, axes, x)]
    dot_general x5 -> x1, matrix products: 76.4 us -> 2.26 us  [local(): lax.dot_general(late_left, shift[:, f:], contract_rows, precision=lax.Pre...]
    unnamed x3 -> x2, waiting for transfers between devices: 0.05 us -> 32 us
    all_gather x2 -> x0, waiting for transfers between devices: 23.8 us -> none  [the longest x1 23.8 us: sent_together(): lax.all_gather(both, axis, axis=dim, tiled=True)]
    reduce_sum x11 -> x3, other arithmetic: 16.8 us -> 1.21 us  [the longest x1 0.6 us: local(): device_count = jnp.sum(window_counts.astype(jnp.float32))]
  transfers between devices with their start and end apart: 3 -> 1, of which waited for: 2 -> 1; matrix products, arithmetic and copies ran while one was open for 15% -> 0% of each run, Pallas kernels for 0% -> 56%
where the time goes in v1:
time: 195 us
  Pallas kernels  130 us (67%)
  waiting for transfers between devices  32 us (16%)
  between operations  14.9 us (8%)
  local copies, waits for them, and re-layouts  10 us (5%)
  other arithmetic  4 us (2%)
  matrix products  2.26 us (1%)
    pallas_call x1, Pallas kernels, product(): pl.pallas_call(functools.partial(product_kernel, widths_of(width)), out_s...  110 us
    unnamed x2, waiting for transfers between devices  32 us
    pallas_call x1, Pallas kernels, center(): pl.pallas_call(center_kernel, grid=(windows,), in_specs=[pl.BlockSpec(mem...  19.9 us
    unnamed x21, local copies, waits for them, and re-layouts  5.43 us
  transfers between devices with their start and end apart: 1, of which 1 were waited for; matrix products, arithmetic and copies ran while one was open for 0% of the time, Pallas kernels for 56%

profile of v1, /device:TPU:0, one launch (start us, length us, event | category | flops | bytes accessed | tf_op | source)
XLA Modules:
  0.0 194.9 jit_solution(3131885857693384969)
XLA Ops:
  7.2 0.0 copy-start.5
  7.2 0.0 all-reduce.3.cloned.1.call-start
  7.2 0.0 copy-start
  7.2 0.6 copy-done
  7.9 0.0 copy-start.1
  7.9 19.9 %center.1 = (bf16[2048,1536]{1,0:T(8,128)(2,1)}, bf16[1536,2048]{1,0:T(8,128)(2,1)}, bf16[2048,128]{1,0:T(8,128)(2,1)S(1)}, bf16[128,2048]{1,0:T(8,128)(2,1)S(1)}, f32[8,2048]{1,0:T(8,128)S(1)}) custom-call(s32[4]{0:T(128)S(1)} %copy-done, bf16[1536,2048]{1,0:T(8,128)(2,1)} %first_ref.1, bf16[1536,2048]{1,0:T(8,128)(2,1)} %second_ref.1), custom_call_target="tpu_custom_call" | custom-call | flops 40000000 | bytes 28000000 | tf_op jit(solution)/shard_map/center/pallas_call | solution.py:90
  27.7 0.0 copy-start.2
  27.7 0.8 copy-done.2
  28.5 0.0 copy-start.3
  28.5 0.8 copy-done.3
  29.4 0.0 copy-done.1
  29.4 0.6 convert_reduce_fusion
  30.0 1.8 all_gather.6
  31.9 0.6 constant_dynamic-update-slice_fusion
  32.6 0.0 copy-done.5
  32.6 0.6 dynamic-slice
  33.8 0.2 broadcast.8
  34.0 0.7 dynamic-update-slice
  34.7 0.0 copy-start.4
  34.8 1.6 copy-done.4
  36.4 0.0 all-reduce.3.cloned.1.call-update
  36.4 110.1 %product.1 = f32[64,2048]{1,0:T(8,128)} custom-call(bf16[32,64,1536]{2,1,0:T(8,128)(2,1)} %bitcast.17, bf16[1536,2048]{1,0:T(8,128)(2,1)} %get-tuple-element.8.right_hbm, bf16[32,64,128]{2,1,0:T(8,128)(2,1)} %bitcast.10, bf16[128,2048]{1,0:T(8,128)(2,1)} %copy-done.3), custom_call_target="tpu_custom_call" | custom-call | flops 27917287424 | bytes 30000000 | tf_op jit(solution)/shard_map/product/pallas_call | solution.py:480
  146.5 32.0 %all-reduce.3.cloned.1.call-done = f32[786496]{0:T(1024)} async-done(((f32[786496]{0:T(1024)}), f32[786496]{0:T(1024)}) %all-reduce.3.cloned.1.call-update) | async-done | bytes 3146000
  178.5 3.8 %reshape.23 = f32[64,12289]{1,0:T(8,128)S(1)} reshape(f32[786496]{0:T(1024)} %all-reduce.3.cloned.1.call-done) | data formatting | bytes 6291968 | tf_op jit(solution)/shard_map/all_gather | solution.py:528
  182.4 0.7 slice_reduce_fusion.1
  183.1 0.3 slice_reduce_fusion
  183.3 0.7 broadcast_divide_fusion
  184.0 0.0 copy-start.6
  184.0 0.3 multiply_reduce_fusion
  184.4 0.7 add_divide_fusion
  185.1 0.1 dynamic-slice_add_fusion
  185.2 0.6 pad_maximum_fusion
  185.8 0.0 copy-done.6
  185.8 2.3 %fusion.1 = f32[64,2048]{1,0:T(8,128)} fusion(f32[64,2048]{1,0:T(8,128)S(1)} %copy-done.6, f32[64,6144]{1,0:T(8,128)S(1)} %get-tuple-element.17, f32[2048]{0:T(1024)S(1)} %slice_add_fusion, f32[64]{0:T(128)S(1)} %dynamic-slice_add_fusion, f32[]{:T(128)} %get-tuple-element.14, s32[]{:T(128)S(6)} %select_n.7, f32[64]{0:T(128)S(1)} %get-tuple-element.15), kind=kOutput, calls=%fused_computation.2 | convolution fusion | flops 101191680 | bytes 1614856 | tf_op jit(solution)/shard_map/dot_general | solution.py:539
  (9 shorter events, 0.1 us)
Async XLA Ops:
  7.2 25.4 %copy-start.5 = (u32[128]{0:T(128)S(1)}, u32[128]{0:T(128)}, u32[]{:S(2)}) copy-start(u32[128]{0:T(128)} %constant.35) | copy-start | bytes 1540
  7.2 171.3 %all-reduce.3.cloned.1.call-start = ((), (), s32[]{:S(2)}) async-start(), calls=%async_computation | async-start | bytes 6299648
  7.2 0.7 copy-start
  7.9 21.5 %copy-start.1 = (s32[4]{0:T(128)S(1)}, s32[4]{0:T(128)}, u32[]{:S(2)}) copy-start(s32[4]{0:T(128)} %counts_ref.1) | copy-start | bytes 52
  27.7 0.8 copy-start.2
  28.5 0.8 copy-start.3
  34.7 1.7 copy-start.4
  184.0 1.8 copy-start.6
Sparse Core Ops, SparseCore 0:
  36.5 141.9 all-reduce.2

commit v2 on v0

v2 whole, which is shorter than its diff:
```python
import functools

import jax
import jax.numpy as jnp
from jax import lax
from jax.experimental import pallas as pl
from jax.experimental.pallas import tpu as pltpu
from jax.sharding import Mesh
from jax.sharding import PartitionSpec as P

TOK = ("tok_0", "tok_1", "tok_2")
MESH = pl.DeviceIdType.MESH
LANE = 128
AUX = 128
CODES = 32767.0

DISTANCES = (2, 1, 3, 0)


def widths_of(width):
    tiles = width // LANE
    return [(tiles // 3 + (1 if q < tiles % 3 else 0)) * LANE for q in range(3)]


def pick(k, values):
    result = values[-1]
    for n in range(len(values) - 2, -1, -1):
        result = jnp.where(k == n, values[n], result)
    return result


def kernel(
    widths,
    counts_ref, first_hbm, second_hbm, out_ref, means_ref,
    raw, left, right, sums, far_out, far_in, near_out, near_in, last_out, last_in, mid_in,
    far_scale, far_scale_in, near_scale, near_scale_in, mid_scale, mid_scale_in, last_scale, last_scale_in,
    means, squares, stats, spread_first, column,
    load_sem, peer_send, peer_recv, stat_send, stat_recv, spread_send, spread_recv,
    far_s, far_r, far_t, far_u, near_s, near_r, near_t, near_u,
    mid_s, mid_r, mid_t, mid_u, last_s, last_r, last_t, last_u,
):
    me = [lax.axis_index(name) for name in TOK]
    core = lax.axis_index("col")
    tokens, width = raw.shape
    slots = tokens // 4
    half_blocks = left.shape[0] // 2
    block = left.shape[1]
    starts = [sum(widths[:q]) for q in range(3)]
    rows = sums.shape[0]
    upper, lower = pl.ds(0, rows // 2), pl.ds(rows // 2, rows // 2)

    def at(axis, coordinate):
        return {TOK[d]: jnp.where(axis == d, coordinate, me[d]) for d in range(3)}

    other = {"col": 1 - core}

    loads = []
    for w in range(4):
        lines = pl.ds(w * slots, slots)
        loads.append(pltpu.make_async_copy(first_hbm.at[lines], raw.at[lines], load_sem.at[0, w]))
    for w in range(4):
        lines = pl.ds(w * slots, slots)
        loads.append(pltpu.make_async_copy(second_hbm.at[lines], right.at[lines], load_sem.at[1, w]))
    for copy in loads:
        copy.start()
    barrier = pltpu.get_barrier_semaphore()
    for d in range(3):
        for step in (1, 2, 3):
            pl.semaphore_signal(
                barrier, inc=1, device_id={TOK[d]: lax.rem(me[d] + step, 4)}, device_id_type=MESH
            )
    pl.semaphore_signal(barrier, inc=1, device_id=other, device_id_type=MESH)

    count = [counts_ref[w].astype(jnp.float32) for w in range(4)]
    device_count = count[0] + count[1] + count[2] + count[3]
    row = lax.broadcasted_iota(jnp.int32, (8, tokens), 0)
    slot = lax.broadcasted_iota(jnp.int32, (8, tokens), 1)
    live_rows = jnp.zeros((8, tokens), jnp.float32)
    for w in range(4):
        inside = (row == w) & (slot >= w * slots) & (slot < w * slots + counts_ref[w])
        live_rows = jnp.where(inside, 1.0, live_rows)
    live_rows = live_rows.astype(jnp.bfloat16)
    eight = lax.broadcasted_iota(jnp.int32, (8, LANE), 0)
    count_rows = jnp.ones((8, LANE), jnp.float32)
    weight_rows = jnp.zeros((8, LANE), jnp.float32)
    for w in range(4):
        count_rows = jnp.where(eight == w, count[w], count_rows)
        weight_rows = jnp.where(eight == w, count[w], weight_rows)

    def cs_of(j):
        return pl.ds(pl.multiple_of(j * LANE, LANE), LANE)

    def loop(n, body):
        def step(j, _):
            body(j)
            return 0

        lax.fori_loop(0, n, step, 0)

    squares[...] = jnp.zeros_like(squares)
    for which, ref in ((0, raw), (1, right)):
        for w in range(4):
            loads[4 * which + w].wait()
        means[which] = jnp.dot(live_rows, ref[pl.ds(0, tokens), :], preferred_element_type=jnp.float32)

    pl.semaphore_wait(barrier, 10)

    def stat_copies(kind, d):
        send, recv = ((stat_send, stat_recv), (spread_send, spread_recv))[kind]
        copies = []
        for step in (1, 2, 3):
            to = lax.rem(me[d] + step, 4)
            copies.append(
                pltpu.make_async_remote_copy(
                    stats.at[kind, d, me[d]], stats.at[kind, d, me[d]], send.at[d, step - 1], recv.at[d, me[d]],
                    device_id={TOK[d]: to}, device_id_type=MESH,
                )
            )
        return copies

    def stat_arrivals(kind, d):
        recv = (stat_recv, spread_recv)[kind]
        send = (stat_send, spread_send)[kind]
        for step in (1, 2, 3):
            source = lax.rem(me[d] + step, 4)
            pltpu.make_async_remote_copy(
                stats.at[kind, d, source], stats.at[kind, d, source], send.at[d, step - 1], recv.at[d, source],
                device_id={TOK[d]: source}, device_id_type=MESH,
            ).wait_recv()

    def stat_sum(kind, d):
        return stats[kind, d, 0] + stats[kind, d, 1] + stats[kind, d, 2] + stats[kind, d, 3]

    def stat_start(kind, d):
        for copy in stat_copies(kind, d):
            copy.start()

    def stat_next(kind, d):
        stat_arrivals(kind, d)
        stats[kind, d + 1, me[d + 1]] = stat_sum(kind, d)
        stat_start(kind, d + 1)

    for which in (0, 1):
        stats[0, 0, me[0], which] = jnp.sum(means[which], axis=0, keepdims=True)
    stats[0, 0, me[0], 2] = jnp.full((1, width), device_count, jnp.float32)
    stat_start(0, 0)

    def to_means(j):
        cs = cs_of(j)
        for which in (0, 1):
            means[which, :, cs] = means[which, :, cs] / count_rows

    loop(width // LANE, to_means)

    mine = pl.ds(core * half_blocks, half_blocks)
    groups = LANE // block

    def push(k, lanes):
        return pltpu.make_async_remote_copy(
            left.at[mine, :, lanes], left.at[mine, :, lanes], peer_send.at[k], peer_recv.at[k],
            device_id=other, device_id_type=MESH,
        )

    def window_push(w):
        return push(w, pl.ds(w * slots, slots))

    def aux_push():
        return push(4, pl.ds(tokens, AUX))

    def center(w):
        live = lax.broadcasted_iota(jnp.int32, (slots, LANE), 0) < counts_ref[w]
        lines = pl.ds(w * slots, slots)

        def centered_of(ref, which, cs):
            mean = means[which, w : w + 1, cs]
            x = jnp.where(live, ref[lines, cs].astype(jnp.float32) - mean, 0.0).astype(jnp.bfloat16)
            wide = x.astype(jnp.float32)
            squares[which, :, cs] += jnp.sum((wide * wide).reshape(slots // 8, 8, LANE), axis=0)
            return x

        def chunk(j):
            cs = cs_of(j)
            turned = centered_of(raw, 0, cs).T
            for k in range(groups):
                left[core * half_blocks + j * groups + k, :, lines] = turned[k * block : (k + 1) * block]
            right[lines, cs] = centered_of(right, 1, cs)

        loop(width // LANE, chunk)
        window_push(w).start()

    center(0)
    stat_next(0, 0)
    center(1)
    stat_next(0, 1)
    center(2)
    stat_arrivals(0, 2)
    total = stat_sum(0, 2)
    grand_count = total[2, 0, 0]
    for which in (0, 1):
        means_ref[which : which + 1, :] = total[which] / total[2]

    row16 = lax.broadcasted_iota(jnp.int32, (16, LANE), 0)

    def aux_rows(which, cs, weighted):
        grand = means_ref[which : which + 1, cs]
        packed = jnp.zeros((16, LANE), jnp.float32)
        for w in range(4):
            value = means[which, w : w + 1, cs] - grand
            if weighted:
                value = count[w] * value
            high = value.astype(jnp.bfloat16).astype(jnp.float32)
            low = value - high
            order = (high, high, low, low) if weighted else (high, low, high, low)
            for k in range(4):
                packed = jnp.where(row16 == 4 * k + w, order[k], packed)
        return jnp.concatenate([packed, jnp.zeros((AUX - 16, LANE), jnp.float32)], axis=0)

    def aux(j):
        cs = cs_of(j)
        turned = aux_rows(0, cs, True).T.astype(jnp.bfloat16)
        for k in range(groups):
            left[core * half_blocks + j * groups + k, :, pl.ds(tokens, AUX)] = turned[k * block : (k + 1) * block]
        right[pl.ds(tokens, AUX), cs] = aux_rows(1, cs, False).astype(jnp.bfloat16)

    loop(width // LANE, aux)
    aux_push().start()
    center(3)

    def spread(j):
        cs = cs_of(j)
        for which in (0, 1):
            shift = means[which, :, cs] - means_ref[which : which + 1, cs]
            part = squares[which, :, cs] + weight_rows * shift * shift
            stats[1, 0, me[0], which, :, cs] = jnp.sum(part, axis=0, keepdims=True)

    stats[1, 0, me[0], 2] = jnp.zeros((1, width), jnp.float32)
    loop(width // LANE, spread)
    stat_start(1, 0)

    pushes = [window_push(w) for w in range(4)] + [aux_push()]
    for copy in pushes:
        copy.wait_recv()

    axes = [[lax.rem(core + q + k, 3) for k in range(3)] for q in range(3)]
    here = [[pick(axes[q][k], me) for k in range(3)] for q in range(3)]
    stride = [[pick(axes[q][k], (16, 4, 1)) for k in range(3)] for q in range(3)]

    def columns(q):
        return pl.ds(starts[q], widths[q])

    def moved(q, k, step):
        return lax.rem(here[q][k] + step, 4)

    def device(q, k, step):
        return at(axes[q][k], moved(q, k, step))

    def distance_of(k):
        return pick(k, DISTANCES)

    def multiply(q, first_step, second_step):
        base = moved(q, 0, first_step) * stride[q][0] + moved(q, 1, second_step) * stride[q][1]
        blocks = [left[base + moved(q, 2, distance) * stride[q][2]] for distance in DISTANCES]
        sums[:, columns(q)] = jnp.dot(
            jnp.concatenate(blocks, axis=0), right[:, columns(q)], preferred_element_type=jnp.float32
        )

    def encoded(p, code_ref, scale_ref):
        peak = jnp.maximum(jnp.max(jnp.abs(p), axis=0, keepdims=True), 1e-30)
        code = jnp.round(p * (CODES / peak)).astype(jnp.int32)
        code_ref[...] = code.astype(jnp.int16)
        scale_ref[...] = peak * (1.0 / CODES)

    def decoded(code_ref, scale_ref):
        return code_ref[...].astype(jnp.int32).astype(jnp.float32) * scale_ref[...]

    def each_tile(q, body):
        def step(j):
            body(pl.ds(pl.multiple_of(starts[q] + j * LANE, LANE), LANE))

        loop(widths[q] // LANE, step)

    def pair(code, code_to, scale, scale_to, sems, index, to):
        s, r, t, u = sems
        return (
            pltpu.make_async_remote_copy(
                code, code_to, s.at[index], r.at[index], device_id=to, device_id_type=MESH
            ),
            pltpu.make_async_remote_copy(
                scale, scale_to, t.at[index], u.at[index], device_id=to, device_id_type=MESH
            ),
        )

    far_sems = (far_s, far_r, far_t, far_u)
    near_sems = (near_s, near_r, near_t, near_u)
    mid_sems = (mid_s, mid_r, mid_t, mid_u)
    last_sems = (last_s, last_r, last_t, last_u)

    def far(q, k, way):
        cs = columns(q)
        lines = (upper, lower)[way]
        return pair(
            far_out.at[k, lines, cs], far_in.at[k, lines, cs],
            far_scale.at[k, :, cs], far_scale_in.at[2 * k + way, :, cs],
            far_sems, (q, 2 * k + way), device(q, 0, (1, 3)[way]),
        )

    def near(q, n, step):
        cs = columns(q)
        return pair(
            near_out.at[n, :, cs], near_in.at[n, :, cs], near_scale.at[n, :, cs], near_scale_in.at[n, :, cs],
            near_sems, (q, n), device(q, 0, step),
        )

    def start(copies):
        for copy in copies:
            copy.start()

    def arrived(copies):
        for copy in copies:
            copy.wait_recv()

    def gone(copies):
        for copy in copies:
            copy.wait_send()

    def serve_far(k):
        for q in range(3):
            multiply(q, 2, distance_of(k))

            def body(cs):
                encoded(sums[:, cs], far_out.at[k, :, cs], far_scale.at[k, :, cs])

            each_tile(q, body)
            start(far(q, k, 0))
            start(far(q, k, 1))

    def serve_near(k):
        for way in (0, 1):
            for q in range(3):
                step = (1, 3)[way]
                multiply(q, step, distance_of(k))
                arrived(far(q, k, way))
                n = 2 * k + way

                def body(cs):
                    p = sums[:, cs]
                    more = decoded(far_in.at[k, (upper, lower)[way], cs], far_scale_in.at[n, :, cs])
                    if way == 0:
                        p = jnp.concatenate([p[: rows // 2] + more, p[rows // 2 :]], axis=0)
                    else:
                        p = jnp.concatenate([p[: rows // 2], p[rows // 2 :] + more], axis=0)
                    encoded(p, near_out.at[n, :, cs], near_scale.at[n, :, cs])

                each_tile(q, body)
                start(near(q, n, step))

    loop(4, serve_far)
    stat_next(1, 0)
    loop(2, serve_near)
    stat_next(1, 1)
    loop(2, lambda k: serve_near(k + 2))
    stat_arrivals(1, 2)
    spread_first[core] = stat_sum(1, 2)
    spread_push = pltpu.make_async_remote_copy(
        spread_first.at[core], spread_first.at[core], peer_send.at[5], peer_recv.at[5],
        device_id=other, device_id_type=MESH,
    )
    spread_push.start()

    def far_gone(k):
        for q in range(3):
            gone(far(q, k, 0))
            gone(far(q, k, 1))

    loop(4, far_gone)
    mid_out = far_out

    def mid(q, n, way=0):
        cs = columns(q)
        lines = (upper, lower)[way] if n == 0 else pl.ds(0, rows)
        k = way if n == 0 else n + 1
        step = (1, 3)[way] if n == 0 else (1, 3)[n - 1]
        return pair(
            mid_out.at[n, lines, cs], mid_in.at[n, lines, cs], mid_scale.at[n, :, cs], mid_scale_in.at[k, :, cs],
            mid_sems, (q, k), device(q, 1, step),
        )

    def merged(k, cs):
        n = 2 * k
        return (
            sums[:, cs]
            + decoded(near_in.at[n, :, cs], near_scale_in.at[n, :, cs])
            + decoded(near_in.at[n + 1, :, cs], near_scale_in.at[n + 1, :, cs])
        )

    def own(k):
        for q in range(3):
            multiply(q, 0, distance_of(k))
            arrived(near(q, 2 * k, 1))
            arrived(near(q, 2 * k + 1, 3))

            @pl.when(k == 0)
            def _():
                def body(cs):
                    encoded(merged(k, cs), mid_out.at[0, :, cs], mid_scale.at[0, :, cs])

                each_tile(q, body)
                start(mid(q, 0, 0))
                start(mid(q, 0, 1))

            @pl.when(k == 1)
            def _():
                arrived(mid(q, 0, 0))

                def body(cs):
                    p = merged(k, cs)
                    more = decoded(mid_in.at[0, upper, cs], mid_scale_in.at[0, :, cs])
                    p = jnp.concatenate([p[: rows // 2] + more, p[rows // 2 :]], axis=0)
                    encoded(p, mid_out.at[1, :, cs], mid_scale.at[1, :, cs])

                each_tile(q, body)
                start(mid(q, 1))

            @pl.when(k == 2)
            def _():
                arrived(mid(q, 0, 1))

                def body(cs):
                    p = merged(k, cs)
                    more = decoded(mid_in.at[0, lower, cs], mid_scale_in.at[1, :, cs])
                    p = jnp.concatenate([p[: rows // 2], p[rows // 2 :] + more], axis=0)
                    encoded(p, mid_out.at[2, :, cs], mid_scale.at[2, :, cs])

                each_tile(q, body)
                start(mid(q, 2))

            @pl.when(k == 3)
            def _():
                def body(cs):
                    sums[:, cs] = merged(k, cs)

                each_tile(q, body)

    loop(4, own)

    part = rows // 4
    half = part // 2
    front, back = pl.ds(0, half), pl.ds(half, half)

    def last(q, n, way=0):
        cs = columns(q)
        lines = (front, back)[way] if n == 0 else pl.ds(0, part)
        k = way if n == 0 else n + 1
        step = (1, 3)[way] if n == 0 else (1, 3)[n - 1]
        return pair(
            last_out.at[n, lines, cs], last_in.at[n, lines, cs], last_scale.at[n, :, cs], last_scale_in.at[k, :, cs],
            last_sems, (q, k), device(q, 2, step),
        )

    for q in range(3):
        arrived(mid(q, 1))
        arrived(mid(q, 2))

        def body(cs):
            p = (
                sums[:, cs]
                + decoded(mid_in.at[1, :, cs], mid_scale_in.at[2, :, cs])
                + decoded(mid_in.at[2, :, cs], mid_scale_in.at[3, :, cs])
            )
            encoded(p[:part], last_out.at[0, :, cs], last_scale.at[0, :, cs])
            sums[pl.ds(part, 3 * part), cs] = p[part:]

        each_tile(q, body)
        start(last(q, 0, 0))
        start(last(q, 0, 1))

    for q in range(3):
        arrived(last(q, 0, 0))
        arrived(last(q, 0, 1))

        def body(cs):
            ahead = jnp.concatenate(
                [
                    sums[pl.ds(part, half), cs] + decoded(last_in.at[0, front, cs], last_scale_in.at[0, :, cs]),
                    sums[pl.ds(part + half, half), cs],
                ],
                axis=0,
            )
            encoded(ahead, last_out.at[1, :, cs], last_scale.at[1, :, cs])
            behind = jnp.concatenate(
                [
                    sums[pl.ds(2 * part, half), cs],
                    sums[pl.ds(2 * part + half, half), cs]
                    + decoded(last_in.at[0, back, cs], last_scale_in.at[1, :, cs]),
                ],
                axis=0,
            )
            encoded(behind, last_out.at[2, :, cs], last_scale.at[2, :, cs])

        each_tile(q, body)
        start(last(q, 1))
        start(last(q, 2))

    spread_push.wait_recv()
    row_block = me[0] * 16 + me[1] * 4 + me[2]
    in_half = lax.rem(row_block, half_blocks)
    lane_block = cs_of(in_half * block // LANE)
    line = spread_first[row_block // half_blocks, 0, :, lane_block] / grand_count
    column[...] = jnp.broadcast_to(line, (LANE, LANE)).T
    rows_var = column[pl.ds(pl.multiple_of(lax.rem(in_half, groups) * block, block), block), :] + 0.1

    for q in range(3):
        arrived(last(q, 1))
        arrived(last(q, 2))

        def body(cs):
            cross = (
                sums[pl.ds(3 * part, part), cs]
                + decoded(last_in.at[1, :, cs], last_scale_in.at[2, :, cs])
                + decoded(last_in.at[2, :, cs], last_scale_in.at[3, :, cs])
            )
            columns_var = spread_first[core, 1, :, cs] / grand_count + 0.1
            out_ref[:, cs] = cross / grand_count * lax.rsqrt(rows_var * columns_var)

        each_tile(q, body)

    def near_gone(k):
        for q in range(3):
            gone(near(q, 2 * k, 1))
            gone(near(q, 2 * k + 1, 3))

    loop(4, near_gone)
    for q in range(3):
        for copies in (mid, last):
            gone(copies(q, 0, 0))
            gone(copies(q, 0, 1))
            gone(copies(q, 1))
            gone(copies(q, 2))
    for copy in pushes + [spread_push]:
        copy.wait_send()
    for kind in (0, 1):
        for d in range(3):
            for copy in stat_copies(kind, d):
                copy.wait_send()


def local(first_acts, second_acts, window_counts):
    tokens, width = first_acts.shape
    block = width * lax.axis_size("col") // lax.axis_size(TOK)
    blocks = width // block
    rows, depth = 4 * block, tokens + AUX
    i16, f32, bf16 = jnp.int16, jnp.float32, jnp.bfloat16
    dma = pltpu.SemaphoreType.DMA
    vmem = pltpu.VMEM
    return pl.pallas_call(
        functools.partial(kernel, widths_of(width)),
        out_shape=(jax.ShapeDtypeStruct((block, width), f32), jax.ShapeDtypeStruct((2, width), f32)),
        in_specs=[
            pl.BlockSpec(memory_space=pltpu.SMEM),
            pl.BlockSpec(memory_space=pl.ANY),
            pl.BlockSpec(memory_space=pl.ANY),
        ],
        out_specs=(pl.BlockSpec(memory_space=vmem), pl.BlockSpec(memory_space=vmem)),
        scratch_shapes=[
            vmem((tokens, width), bf16),
            vmem((2 * blocks, block, depth), bf16),
            vmem((depth, width), bf16),
            vmem((rows, width), f32),
            vmem((4, rows, width), i16), vmem((4, rows, width), i16),
            vmem((8, rows, width), i16), vmem((8, rows, width), i16),
            vmem((3, block, width), i16), vmem((3, block, width), i16),
            vmem((3, rows, width), i16),
            vmem((4, 1, width), f32), vmem((8, 1, width), f32),
            vmem((8, 1, width), f32), vmem((8, 1, width), f32),
            vmem((3, 1, width), f32), vmem((4, 1, width), f32),
            vmem((3, 1, width), f32), vmem((4, 1, width), f32),
            vmem((2, 8, width), f32), vmem((2, 8, width), f32),
            vmem((2, 3, 4, 3, 1, width), f32),
            vmem((2, 3, 1, width), f32),
            vmem((LANE, LANE), f32),
            dma((2, 4)), dma((6,)), dma((6,)),
            dma((3, 3)), dma((3, 4)), dma((3, 3)), dma((3, 4)),
            dma((3, 8)), dma((3, 8)), dma((3, 8)), dma((3, 8)),
            dma((3, 8)), dma((3, 8)), dma((3, 8)), dma((3, 8)),
            dma((3, 4)), dma((3, 4)), dma((3, 4)), dma((3, 4)),
            dma((3, 4)), dma((3, 4)), dma((3, 4)), dma((3, 4)),
        ],
        compiler_params=pltpu.CompilerParams(
            collective_id=0, has_side_effects=True, vmem_limit_bytes=67_043_328
        ),
        cost_estimate=pl.CostEstimate(
            flops=4 * width * width * depth, bytes_accessed=30_000_000, transcendentals=0
        ),
        name="whole",
    )(window_counts, first_acts, second_acts)


def solution(mesh):
    torus = Mesh(
        mesh.devices.reshape(4, 4, 4, mesh.shape["col"]), ("tok_0", "tok_1", "tok_2", "col")
    )
    return jax.shard_map(
        local,
        mesh=torus,
        in_specs=(P(TOK, "col"), P(TOK, "col"), P(TOK)),
        out_specs=(P(TOK, "col"), P(None, "col")),
        check_vma=False,
    )
```

time: 567 us -> 121 us (0.21)
  waiting for transfers between devices: 364 us -> 0 us
  Pallas kernels: 0 us -> 116 us
  blocking collectives: 83.8 us -> 0 us
  matrix products: 76.4 us -> 0 us
  other arithmetic: 25 us -> 0 us
  between operations: 13.9 us -> 0.64 us
    reduce_scatter x1 -> x0, waiting for transfers between devices: 340 us -> none  [local(): lax.psum_scatter(product + lax.dot_general(early_left, shift_second, cont...]
    pallas_call x0 -> x1, Pallas kernels: none -> 116 us  [local(): pl.pallas_call(functools.partial(kernel, widths_of(width)), out_shape=(ja...]
    psum x3 -> x0, blocking collectives: 80 us -> none  [one_axis_at_a_time(): return functools.reduce(lax.psum, axes, x)]
    dot_general x5 -> x0, matrix products: 76.4 us -> none  [the longest x1 37.9 us: local(): lax.dot_general(whole_first, centered_second, contract_rows, preferred_el...]
    all_gather x2 -> x0, waiting for transfers between devices: 23.8 us -> none  [the longest x1 23.8 us: sent_together(): lax.all_gather(both, axis, axis=dim, tiled=True)]
    reduce_sum x12 -> x0, other arithmetic: 17.5 us -> none  [the longest x1 7.52 us: local(): square_first = jnp.sum(jnp.square(whole_first.astype(jnp.float32)), axis=0)]
  transfers between devices with their start and end apart: 3 -> 0, of which waited for: 2 -> 0; matrix products, arithmetic and copies ran while one was open for 15% -> 0% of each run, Pallas kernels for 0% -> 0%
where the time goes in v2:
time: 121 us; the launch traced here: 119 us
  Pallas kernels  116 us (96%)
  local copies, waits for them, and re-layouts  3.2 us (3%)
    pallas_call x1, Pallas kernels, local(): pl.pallas_call(functools.partial(kernel, widths_of(width)), out_shape=(ja...  116 us
    unnamed x2, local copies, waits for them, and re-layouts  3.2 us

profile of v2, /device:TPU:0, one launch (start us, length us, event | category | flops | bytes accessed | tf_op | source)
XLA Modules:
  0.0 119.5 jit_solution(16708002351780296604)
XLA Ops:
  0.6 115.7 %whole.1 = (f32[64,2048]{1,0:T(8,128)}, f32[2,2048]{1,0:T(2,128)}) custom-call(s32[4]{0:T(128)} %counts_ref.1, bf16[1536,2048]{1,0:T(8,128)(2,1)} %first_hbm.1, bf16[1536,2048]{1,0:T(8,128)(2,1)} %second_hbm.1), custom_call_target="tpu_custom_call" | custom-call | flops 27917287424 | bytes 30000000 | tf_op jit(solution)/shard_map/whole/pallas_call | solution.py:555
  116.3 1.9 %copy.7 = f32[64,2048]{1,0:T(8,128)} copy(f32[64,2048]{1,0:T(8,128)} %get-tuple-element.4) | data formatting | bytes 1048576
  118.2 1.3 %copy.8 = f32[2,2048]{1,0:T(2,128)} copy(f32[2,2048]{1,0:T(2,128)} %get-tuple-element.5) | data formatting | bytes 32768

commit v3 on v0

v3 whole, which is shorter than its diff:
```python
import functools

import jax
import jax.numpy as jnp
from jax import lax
from jax.experimental import pallas as pl
from jax.experimental.pallas import tpu as pltpu
from jax.sharding import Mesh
from jax.sharding import PartitionSpec as P

TOK = ("tok_0", "tok_1", "tok_2")
MESH = pl.DeviceIdType.MESH
LANE = 128
AUX = 128
CODES = 32767.0

DISTANCES = (2, 1, 3, 0)


def widths_of(width):
    tiles = width // LANE
    return [(tiles // 3 + (1 if q < tiles % 3 else 0)) * LANE for q in range(3)]


def pick(k, values):
    result = values[-1]
    for n in range(len(values) - 2, -1, -1):
        result = jnp.where(k == n, values[n], result)
    return result


def kernel(
    widths,
    counts_ref, first_hbm, second_hbm, out_ref, means_ref,
    left, right, far_out, far_in, near_out, near_in, last_out, last_in, mid_in,
    far_scale, far_scale_in, near_scale, near_scale_in, mid_scale, mid_scale_in, last_scale, last_scale_in,
    means, squares, stats, spread_first, column,
    load_sem, peer_send, peer_recv, stat_send, stat_recv, spread_send, spread_recv,
    far_s, far_r, far_t, far_u, near_s, near_r, near_t, near_u,
    mid_s, mid_r, mid_t, mid_u, last_s, last_r, last_t, last_u,
):
    me = [lax.axis_index(name) for name in TOK]
    core = lax.axis_index("col")
    width = right.shape[1]
    tokens = right.shape[0] - AUX
    slots = tokens // 4
    half_blocks = left.shape[0] // 2
    block = left.shape[1]
    starts = [sum(widths[:q]) for q in range(3)]
    rows = far_out.shape[1]
    upper, lower = pl.ds(0, rows // 2), pl.ds(rows // 2, rows // 2)

    def at(axis, coordinate):
        return {TOK[d]: jnp.where(axis == d, coordinate, me[d]) for d in range(3)}

    other = {"col": 1 - core}

    def cs_of(j):
        return pl.ds(pl.multiple_of(j * LANE, LANE), LANE)

    def loop(n, body):
        def step(j, _):
            body(j)
            return 0

        lax.fori_loop(0, n, step, 0)

    def stat_copies(kind, d):
        send, recv = ((stat_send, stat_recv), (spread_send, spread_recv))[kind]
        copies = []
        for step in (1, 2, 3):
            to = lax.rem(me[d] + step, 4)
            copies.append(
                pltpu.make_async_remote_copy(
                    stats.at[kind, d, me[d]], stats.at[kind, d, me[d]], send.at[d, step - 1], recv.at[d, me[d]],
                    device_id={TOK[d]: to}, device_id_type=MESH,
                )
            )
        return copies

    def stat_arrivals(kind, d):
        recv = (stat_recv, spread_recv)[kind]
        send = (stat_send, spread_send)[kind]
        for step in (1, 2, 3):
            source = lax.rem(me[d] + step, 4)
            pltpu.make_async_remote_copy(
                stats.at[kind, d, source], stats.at[kind, d, source], send.at[d, step - 1], recv.at[d, source],
                device_id={TOK[d]: source}, device_id_type=MESH,
            ).wait_recv()

    def stat_sum(kind, d):
        return stats[kind, d, 0] + stats[kind, d, 1] + stats[kind, d, 2] + stats[kind, d, 3]

    def stat_start(kind, d):
        for copy in stat_copies(kind, d):
            copy.start()

    def stat_next(kind, d):
        stat_arrivals(kind, d)
        stats[kind, d + 1, me[d + 1]] = stat_sum(kind, d)
        stat_start(kind, d + 1)

    mine = pl.ds(core * half_blocks, half_blocks)
    groups = LANE // block

    def push(k, lanes):
        return pltpu.make_async_remote_copy(
            left.at[mine, :, lanes], left.at[mine, :, lanes], peer_send.at[k], peer_recv.at[k],
            device_id=other, device_id_type=MESH,
        )

    def window_push(w):
        return push(w, pl.ds(w * slots, slots))

    def aux_push():
        return push(4, pl.ds(tokens, AUX))

    pushes = [window_push(w) for w in range(4)] + [aux_push()]

    def prepare(raw):
        loads = []
        for w in range(4):
            lines = pl.ds(w * slots, slots)
            loads.append(pltpu.make_async_copy(first_hbm.at[lines], raw.at[lines], load_sem.at[0, w]))
        for w in range(4):
            lines = pl.ds(w * slots, slots)
            loads.append(pltpu.make_async_copy(second_hbm.at[lines], right.at[lines], load_sem.at[1, w]))
        for copy in loads:
            copy.start()
        barrier = pltpu.get_barrier_semaphore()
        for d in range(3):
            for step in (1, 2, 3):
                pl.semaphore_signal(
                    barrier, inc=1, device_id={TOK[d]: lax.rem(me[d] + step, 4)}, device_id_type=MESH
                )
        pl.semaphore_signal(barrier, inc=1, device_id=other, device_id_type=MESH)

        count = [counts_ref[w].astype(jnp.float32) for w in range(4)]
        device_count = count[0] + count[1] + count[2] + count[3]
        row = lax.broadcasted_iota(jnp.int32, (8, tokens), 0)
        slot = lax.broadcasted_iota(jnp.int32, (8, tokens), 1)
        live_rows = jnp.zeros((8, tokens), jnp.float32)
        for w in range(4):
            inside = (row == w) & (slot >= w * slots) & (slot < w * slots + counts_ref[w])
            live_rows = jnp.where(inside, 1.0, live_rows)
        live_rows = live_rows.astype(jnp.bfloat16)
        eight = lax.broadcasted_iota(jnp.int32, (8, LANE), 0)
        count_rows = jnp.ones((8, LANE), jnp.float32)
        weight_rows = jnp.zeros((8, LANE), jnp.float32)
        for w in range(4):
            count_rows = jnp.where(eight == w, count[w], count_rows)
            weight_rows = jnp.where(eight == w, count[w], weight_rows)

        squares[...] = jnp.zeros_like(squares)
        for which, ref in ((0, raw), (1, right)):
            for w in range(4):
                loads[4 * which + w].wait()
            means[which] = jnp.dot(live_rows, ref[pl.ds(0, tokens), :], preferred_element_type=jnp.float32)

        pl.semaphore_wait(barrier, 10)

        for which in (0, 1):
            stats[0, 0, me[0], which] = jnp.sum(means[which], axis=0, keepdims=True)
        stats[0, 0, me[0], 2] = jnp.full((1, width), device_count, jnp.float32)
        stat_start(0, 0)

        def to_means(j):
            cs = cs_of(j)
            for which in (0, 1):
                means[which, :, cs] = means[which, :, cs] / count_rows

        loop(width // LANE, to_means)

        def center(w):
            live = lax.broadcasted_iota(jnp.int32, (slots, LANE), 0) < counts_ref[w]
            lines = pl.ds(w * slots, slots)

            def centered_of(ref, which, cs):
                mean = means[which, w : w + 1, cs]
                x = jnp.where(live, ref[lines, cs].astype(jnp.float32) - mean, 0.0).astype(jnp.bfloat16)
                wide = x.astype(jnp.float32)
                squares[which, :, cs] += jnp.sum((wide * wide).reshape(slots // 8, 8, LANE), axis=0)
                return x

            def chunk(j):
                cs = cs_of(j)
                turned = centered_of(raw, 0, cs).T
                for k in range(groups):
                    left[core * half_blocks + j * groups + k, :, lines] = turned[k * block : (k + 1) * block]
                right[lines, cs] = centered_of(right, 1, cs)

            loop(width // LANE, chunk)
            window_push(w).start()

        center(0)
        stat_next(0, 0)
        center(1)
        stat_next(0, 1)
        center(2)
        stat_arrivals(0, 2)
        total = stat_sum(0, 2)
        for which in (0, 1):
            means_ref[which : which + 1, :] = total[which] / total[2]

        row16 = lax.broadcasted_iota(jnp.int32, (16, LANE), 0)

        def aux_rows(which, cs, weighted):
            grand = means_ref[which : which + 1, cs]
            packed = jnp.zeros((16, LANE), jnp.float32)
            for w in range(4):
                value = means[which, w : w + 1, cs] - grand
                if weighted:
                    value = count[w] * value
                high = value.astype(jnp.bfloat16).astype(jnp.float32)
                low = value - high
                order = (high, high, low, low) if weighted else (high, low, high, low)
                for k in range(4):
                    packed = jnp.where(row16 == 4 * k + w, order[k], packed)
            return jnp.concatenate([packed, jnp.zeros((AUX - 16, LANE), jnp.float32)], axis=0)

        def aux(j):
            cs = cs_of(j)
            turned = aux_rows(0, cs, True).T.astype(jnp.bfloat16)
            for k in range(groups):
                left[core * half_blocks + j * groups + k, :, pl.ds(tokens, AUX)] = turned[k * block : (k + 1) * block]
            right[pl.ds(tokens, AUX), cs] = aux_rows(1, cs, False).astype(jnp.bfloat16)

        loop(width // LANE, aux)
        aux_push().start()
        center(3)

        def spread(j):
            cs = cs_of(j)
            for which in (0, 1):
                shift = means[which, :, cs] - means_ref[which : which + 1, cs]
                part = squares[which, :, cs] + weight_rows * shift * shift
                stats[1, 0, me[0], which, :, cs] = jnp.sum(part, axis=0, keepdims=True)

        stats[1, 0, me[0], 2] = jnp.zeros((1, width), jnp.float32)
        loop(width // LANE, spread)
        stat_start(1, 0)

        for copy in pushes:
            copy.wait_recv()

    def reduce(acc):
        sums = acc.at[3]
        axes = [[lax.rem(core + q + k, 3) for k in range(3)] for q in range(3)]
        here = [[pick(axes[q][k], me) for k in range(3)] for q in range(3)]
        stride = [[pick(axes[q][k], (16, 4, 1)) for k in range(3)] for q in range(3)]

        def columns(q):
            return pl.ds(starts[q], widths[q])

        def moved(q, k, step):
            return lax.rem(here[q][k] + step, 4)

        def device(q, k, step):
            return at(axes[q][k], moved(q, k, step))

        def distance_of(k):
            return pick(k, DISTANCES)

        def multiply(q, first_step, second_step, into=None):
            base = moved(q, 0, first_step) * stride[q][0] + moved(q, 1, second_step) * stride[q][1]
            blocks = [left[base + moved(q, 2, distance) * stride[q][2]] for distance in DISTANCES]
            into = sums if into is None else into
            into[:, columns(q)] = jnp.dot(
                jnp.concatenate(blocks, axis=0), right[:, columns(q)], preferred_element_type=jnp.float32
            )

        def encoded(p, code_ref, scale_ref):
            peak = jnp.maximum(jnp.max(jnp.abs(p), axis=0, keepdims=True), 1e-30)
            code = jnp.round(p * (CODES / peak)).astype(jnp.int32)
            code_ref[...] = code.astype(jnp.int16)
            scale_ref[...] = peak * (1.0 / CODES)

        def encode_sums(q, code_ref, scale_ref):
            for cs in tiles(q):
                encoded(sums[:, cs], code_ref.at[:, cs], scale_ref.at[:, cs])

        def tiles(q):
            return [pl.ds(starts[q] + j, LANE) for j in range(0, widths[q], LANE)]

        def decoded(code_ref, scale_ref):
            return code_ref[...].astype(jnp.int32).astype(jnp.float32) * scale_ref[...]

        def each_tile(q, body):
            def step(j):
                body(pl.ds(pl.multiple_of(starts[q] + j * LANE, LANE), LANE))

            loop(widths[q] // LANE, step)

        def pair(code, code_to, scale, scale_to, sems, index, to):
            s, r, t, u = sems
            return (
                pltpu.make_async_remote_copy(
                    code, code_to, s.at[index], r.at[index], device_id=to, device_id_type=MESH
                ),
                pltpu.make_async_remote_copy(
                    scale, scale_to, t.at[index], u.at[index], device_id=to, device_id_type=MESH
                ),
            )

        far_sems = (far_s, far_r, far_t, far_u)
        near_sems = (near_s, near_r, near_t, near_u)
        mid_sems = (mid_s, mid_r, mid_t, mid_u)
        last_sems = (last_s, last_r, last_t, last_u)

        def far(q, k, way):
            cs = columns(q)
            lines = (upper, lower)[way]
            return pair(
                far_out.at[k, lines, cs], far_in.at[k, lines, cs],
                far_scale.at[k, :, cs], far_scale_in.at[2 * k + way, :, cs],
                far_sems, (q, 2 * k + way), device(q, 0, (1, 3)[way]),
            )

        def near(q, n, step):
            cs = columns(q)
            return pair(
                near_out.at[n, :, cs], near_in.at[n, :, cs], near_scale.at[n, :, cs], near_scale_in.at[n, :, cs],
                near_sems, (q, n), device(q, 0, step),
            )

        def start(copies):
            for copy in copies:
                copy.start()

        def arrived(copies):
            for copy in copies:
                copy.wait_recv()

        def gone(copies):
            for copy in copies:
                copy.wait_send()

        def serve_far(k):
            for q in range(3):
                if q < 2:
                    multiply(q + 1, 2, distance_of(k))
                else:
                    multiply(0, jnp.where(k == 3, 1, 2), pick(k, DISTANCES[1:] + DISTANCES[:1]))
                encode_sums(q, far_out.at[k], far_scale.at[k])
                start(far(q, k, 0))
                start(far(q, k, 1))

        def serve_near(k):
            for way in (0, 1):
                n = 2 * k + way
                for q in range(3):
                    arrived(far(q, k, way))
                    if q < 2:
                        multiply(q + 1, (1, 3)[way], distance_of(k))
                    elif way == 0:
                        multiply(0, 3, distance_of(k))
                    else:
                        multiply(0, jnp.where(k == 3, 0, 1), pick(k, DISTANCES[1:] + DISTANCES[3:]))
                    for cs in tiles(q):
                        p = sums[:, cs]
                        more = decoded(far_in.at[k, (upper, lower)[way], cs], far_scale_in.at[n, :, cs])
                        if way == 0:
                            p = jnp.concatenate([p[: rows // 2] + more, p[rows // 2 :]], axis=0)
                        else:
                            p = jnp.concatenate([p[: rows // 2], p[rows // 2 :] + more], axis=0)
                        encoded(p, near_out.at[n, :, cs], near_scale.at[n, :, cs])
                    start(near(q, n, (1, 3)[way]))

        multiply(0, 2, DISTANCES[0])
        loop(4, serve_far)
        stat_next(1, 0)
        def far_gone(k):
            for q in range(3):
                gone(far(q, k, 0))
                gone(far(q, k, 1))

        mid_out = far_out

        def mid(q, n, way=0):
            cs = columns(q)
            lines = (upper, lower)[way] if n == 0 else pl.ds(0, rows)
            k = way if n == 0 else n + 1
            step = (1, 3)[way] if n == 0 else (1, 3)[n - 1]
            return pair(
                mid_out.at[n, lines, cs], mid_in.at[n, lines, cs], mid_scale.at[n, :, cs], mid_scale_in.at[k, :, cs],
                mid_sems, (q, k), device(q, 1, step),
            )

        def merged(k, cs):
            n = 2 * k
            return (
                acc[k, :, cs]
                + decoded(near_in.at[n, :, cs], near_scale_in.at[n, :, cs])
                + decoded(near_in.at[n + 1, :, cs], near_scale_in.at[n + 1, :, cs])
            )

        def take_own(k):
            for q in range(3):
                arrived(near(q, 2 * k, 1))
                arrived(near(q, 2 * k + 1, 3))
                if k in (1, 2):
                    arrived(mid(q, 0, k - 1))

                def body(cs):
                    p = merged(k, cs)
                    if k == 3:
                        sums[:, cs] = p
                        return
                    if k == 1:
                        more = decoded(mid_in.at[0, upper, cs], mid_scale_in.at[0, :, cs])
                        p = jnp.concatenate([p[: rows // 2] + more, p[rows // 2 :]], axis=0)
                    if k == 2:
                        more = decoded(mid_in.at[0, lower, cs], mid_scale_in.at[1, :, cs])
                        p = jnp.concatenate([p[: rows // 2], p[rows // 2 :] + more], axis=0)
                    encoded(p, mid_out.at[k, :, cs], mid_scale.at[k, :, cs])

                each_tile(q, body)
                if k == 0:
                    start(mid(q, 0, 0))
                    start(mid(q, 0, 1))
                elif k < 3:
                    start(mid(q, k))

        def serve(k):
            serve_near(k)

            @pl.when(k == 0)
            def _():
                stat_next(1, 1)
                loop(4, far_gone)

            @pl.when(k >= 1)
            def _():
                for q in range(3):
                    multiply(q, 0, distance_of(k - 1), acc.at[k - 1])

            for before in range(3):

                @pl.when(k == before + 1)
                def _():
                    take_own(before)

        loop(4, serve)
        for q in (1, 2):
            multiply(q, 0, 0)
        take_own(3)
        stat_arrivals(1, 2)
        spread_first[core] = stat_sum(1, 2)
        spread_push = pltpu.make_async_remote_copy(
            spread_first.at[core], spread_first.at[core], peer_send.at[5], peer_recv.at[5],
            device_id=other, device_id_type=MESH,
        )
        spread_push.start()

        part = rows // 4
        half = part // 2
        front, back = pl.ds(0, half), pl.ds(half, half)

        def last(q, n, way=0):
            cs = columns(q)
            lines = (front, back)[way] if n == 0 else pl.ds(0, part)
            k = way if n == 0 else n + 1
            step = (1, 3)[way] if n == 0 else (1, 3)[n - 1]
            return pair(
                last_out.at[n, lines, cs], last_in.at[n, lines, cs], last_scale.at[n, :, cs], last_scale_in.at[k, :, cs],
                last_sems, (q, k), device(q, 2, step),
            )

        for q in range(3):
            arrived(mid(q, 1))
            arrived(mid(q, 2))

            def body(cs):
                p = (
                    sums[:, cs]
                    + decoded(mid_in.at[1, :, cs], mid_scale_in.at[2, :, cs])
                    + decoded(mid_in.at[2, :, cs], mid_scale_in.at[3, :, cs])
                )
                encoded(p[:part], last_out.at[0, :, cs], last_scale.at[0, :, cs])
                sums[pl.ds(part, 3 * part), cs] = p[part:]

            each_tile(q, body)
            start(last(q, 0, 0))
            start(last(q, 0, 1))

        for q in range(3):
            arrived(last(q, 0, 0))
            arrived(last(q, 0, 1))

            def body(cs):
                ahead = jnp.concatenate(
                    [
                        sums[pl.ds(part, half), cs] + decoded(last_in.at[0, front, cs], last_scale_in.at[0, :, cs]),
                        sums[pl.ds(part + half, half), cs],
                    ],
                    axis=0,
                )
                encoded(ahead, last_out.at[1, :, cs], last_scale.at[1, :, cs])
                behind = jnp.concatenate(
                    [
                        sums[pl.ds(2 * part, half), cs],
                        sums[pl.ds(2 * part + half, half), cs]
                        + decoded(last_in.at[0, back, cs], last_scale_in.at[1, :, cs]),
                    ],
                    axis=0,
                )
                encoded(behind, last_out.at[2, :, cs], last_scale.at[2, :, cs])

            each_tile(q, body)
            start(last(q, 1))
            start(last(q, 2))

        spread_push.wait_recv()
        grand_count = stat_sum(0, 2)[2, 0, 0]
        row_block = me[0] * 16 + me[1] * 4 + me[2]
        in_half = lax.rem(row_block, half_blocks)
        lane_block = cs_of(in_half * block // LANE)
        line = spread_first[row_block // half_blocks, 0, :, lane_block] / grand_count
        column[...] = jnp.broadcast_to(line, (LANE, LANE)).T
        rows_var = column[pl.ds(pl.multiple_of(lax.rem(in_half, groups) * block, block), block), :] + 0.1

        for q in range(3):
            arrived(last(q, 1))
            arrived(last(q, 2))

            def body(cs):
                cross = (
                    sums[pl.ds(3 * part, part), cs]
                    + decoded(last_in.at[1, :, cs], last_scale_in.at[2, :, cs])
                    + decoded(last_in.at[2, :, cs], last_scale_in.at[3, :, cs])
                )
                columns_var = spread_first[core, 1, :, cs] / grand_count + 0.1
                out_ref[:, cs] = cross / grand_count * lax.rsqrt(rows_var * columns_var)

            each_tile(q, body)

        def near_gone(k):
            for q in range(3):
                gone(near(q, 2 * k, 1))
                gone(near(q, 2 * k + 1, 3))

        loop(4, near_gone)
        for q in range(3):
            for copies in (mid, last):
                gone(copies(q, 0, 0))
                gone(copies(q, 0, 1))
                gone(copies(q, 1))
                gone(copies(q, 2))
        for copy in pushes + [spread_push]:
            copy.wait_send()
        for kind in (0, 1):
            for d in range(3):
                for copy in stat_copies(kind, d):
                    copy.wait_send()

    pl.run_scoped(prepare, pltpu.VMEM((tokens, width), jnp.bfloat16))
    pl.run_scoped(reduce, pltpu.VMEM((4, rows, width), jnp.float32))


def local(first_acts, second_acts, window_counts):
    tokens, width = first_acts.shape
    block = width * lax.axis_size("col") // lax.axis_size(TOK)
    blocks = width // block
    rows, depth = 4 * block, tokens + AUX
    i16, f32, bf16 = jnp.int16, jnp.float32, jnp.bfloat16
    dma = pltpu.SemaphoreType.DMA
    vmem = pltpu.VMEM
    return pl.pallas_call(
        functools.partial(kernel, widths_of(width)),
        out_shape=(jax.ShapeDtypeStruct((block, width), f32), jax.ShapeDtypeStruct((2, width), f32)),
        in_specs=[
            pl.BlockSpec(memory_space=pltpu.SMEM),
            pl.BlockSpec(memory_space=pl.ANY),
            pl.BlockSpec(memory_space=pl.ANY),
        ],
        out_specs=(pl.BlockSpec(memory_space=vmem), pl.BlockSpec(memory_space=vmem)),
        scratch_shapes=[
            vmem((2 * blocks, block, depth), bf16),
            vmem((depth, width), bf16),
            vmem((4, rows, width), i16), vmem((4, rows, width), i16),
            vmem((8, rows, width), i16), vmem((8, rows, width), i16),
            vmem((3, block, width), i16), vmem((3, block, width), i16),
            vmem((3, rows, width), i16),
            vmem((4, 1, width), f32), vmem((8, 1, width), f32),
            vmem((8, 1, width), f32), vmem((8, 1, width), f32),
            vmem((3, 1, width), f32), vmem((4, 1, width), f32),
            vmem((3, 1, width), f32), vmem((4, 1, width), f32),
            vmem((2, 8, width), f32), vmem((2, 8, width), f32),
            vmem((2, 3, 4, 3, 1, width), f32),
            vmem((2, 3, 1, width), f32),
            vmem((LANE, LANE), f32),
            dma((2, 4)), dma((6,)), dma((6,)),
            dma((3, 3)), dma((3, 4)), dma((3, 3)), dma((3, 4)),
            dma((3, 8)), dma((3, 8)), dma((3, 8)), dma((3, 8)),
            dma((3, 8)), dma((3, 8)), dma((3, 8)), dma((3, 8)),
            dma((3, 4)), dma((3, 4)), dma((3, 4)), dma((3, 4)),
            dma((3, 4)), dma((3, 4)), dma((3, 4)), dma((3, 4)),
        ],
        compiler_params=pltpu.CompilerParams(
            collective_id=0, has_side_effects=True, vmem_limit_bytes=67_043_328
        ),
        cost_estimate=pl.CostEstimate(
            flops=4 * width * width * depth, bytes_accessed=30_000_000, transcendentals=0
        ),
        name="whole",
    )(window_counts, first_acts, second_acts)


def solution(mesh):
    torus = Mesh(
        mesh.devices.reshape(4, 4, 4, mesh.shape["col"]), ("tok_0", "tok_1", "tok_2", "col")
    )
    return jax.shard_map(
        local,
        mesh=torus,
        in_specs=(P(TOK, "col"), P(TOK, "col"), P(TOK)),
        out_specs=(P(TOK, "col"), P(None, "col")),
        check_vma=False,
    )
```

time: 567 us -> 112 us (0.20)
  waiting for transfers between devices: 364 us -> 0 us
  Pallas kernels: 0 us -> 107 us
  blocking collectives: 83.8 us -> 0 us
  matrix products: 76.4 us -> 0 us
  other arithmetic: 25 us -> 0 us
  between operations: 13.9 us -> 0.64 us
    reduce_scatter x1 -> x0, waiting for transfers between devices: 340 us -> none  [local(): lax.psum_scatter(product + lax.dot_general(early_left, shift_second, cont...]
    pallas_call x0 -> x1, Pallas kernels: none -> 107 us  [local(): pl.pallas_call(functools.partial(kernel, widths_of(width)), out_shape=(ja...]
    psum x3 -> x0, blocking collectives: 80 us -> none  [one_axis_at_a_time(): return functools.reduce(lax.psum, axes, x)]
    dot_general x5 -> x0, matrix products: 76.4 us -> none  [the longest x1 37.9 us: local(): lax.dot_general(whole_first, centered_second, contract_rows, preferred_el...]
    all_gather x2 -> x0, waiting for transfers between devices: 23.8 us -> none  [the longest x1 23.8 us: sent_together(): lax.all_gather(both, axis, axis=dim, tiled=True)]
    reduce_sum x12 -> x0, other arithmetic: 17.5 us -> none  [the longest x1 7.52 us: local(): square_first = jnp.sum(jnp.square(whole_first.astype(jnp.float32)), axis=0)]
  transfers between devices with their start and end apart: 3 -> 0, of which waited for: 2 -> 0; matrix products, arithmetic and copies ran while one was open for 15% -> 0% of each run, Pallas kernels for 0% -> 0%
where the time goes in v3:
time: 112 us; the launch traced here: 110 us
  Pallas kernels  107 us (96%)
  local copies, waits for them, and re-layouts  3.2 us (3%)
    pallas_call x1, Pallas kernels, local(): pl.pallas_call(functools.partial(kernel, widths_of(width)), out_shape=(ja...  107 us
    unnamed x2, local copies, waits for them, and re-layouts  3.2 us

profile of v3, /device:TPU:0, one launch (start us, length us, event | category | flops | bytes accessed | tf_op | source)
XLA Modules:
  0.0 110.5 jit_solution(1017141436104210169)
XLA Ops:
  0.6 106.6 %whole.1 = (f32[64,2048]{1,0:T(8,128)}, f32[2,2048]{1,0:T(2,128)}) custom-call(s32[4]{0:T(128)} %counts_ref.1, bf16[1536,2048]{1,0:T(8,128)(2,1)} %first_hbm.1, bf16[1536,2048]{1,0:T(8,128)(2,1)} %second_hbm.1), custom_call_target="tpu_custom_call" | custom-call | flops 27917287424 | bytes 30000000 | tf_op jit(solution)/shard_map/whole/pallas_call | solution.py:568
  107.3 1.9 %copy.7 = f32[64,2048]{1,0:T(8,128)} copy(f32[64,2048]{1,0:T(8,128)} %get-tuple-element.4) | data formatting | bytes 1048576
  109.2 1.3 %copy.8 = f32[2,2048]{1,0:T(2,128)} copy(f32[2,2048]{1,0:T(2,128)} %get-tuple-element.5) | data formatting | bytes 32768

commit v4 on v3

v4 whole, which is shorter than its diff:
```python
import functools

import jax
import jax.numpy as jnp
from jax import lax
from jax.experimental import pallas as pl
from jax.experimental.pallas import tpu as pltpu
from jax.sharding import Mesh
from jax.sharding import PartitionSpec as P

TOK = ("tok_0", "tok_1", "tok_2")
MESH = pl.DeviceIdType.MESH
LANE = 128
AUX = 128
CODES = 32767.0

DISTANCES = (2, 1, 3, 0)


def widths_of(width):
    tiles = width // LANE
    return [(tiles // 3 + (1 if q < tiles % 3 else 0)) * LANE for q in range(3)]


def pick(k, values):
    result = values[-1]
    for n in range(len(values) - 2, -1, -1):
        result = jnp.where(k == n, values[n], result)
    return result


def kernel(
    widths,
    counts_ref, first_hbm, second_hbm, out_ref,
    left, right, far_out, far_in, near_out, near_in, last_out, last_in, mid_in,
    far_scale, far_scale_in, near_scale, near_scale_in, mid_scale, mid_scale_in, last_scale, last_scale_in,
    sums_of, squares, rings, stats, spread_first, grand, column,
    load_sem, peer_send, peer_recv, ring_send, ring_recv, stat_send, stat_recv,
    far_s, far_r, far_t, far_u, near_s, near_r, near_t, near_u,
    mid_s, mid_r, mid_t, mid_u, last_s, last_r, last_t, last_u,
):
    me = [lax.axis_index(name) for name in TOK]
    core = lax.axis_index("col")
    width = right.shape[1]
    tokens = first_hbm.shape[0]
    depth = tokens + AUX
    slots = tokens // 4
    half_blocks = left.shape[0] // 2
    block = left.shape[1]
    starts = [sum(widths[:q]) for q in range(3)]
    rows = far_out.shape[1]
    upper, lower = pl.ds(0, rows // 2), pl.ds(rows // 2, rows // 2)

    def at(axis, coordinate):
        return {TOK[d]: jnp.where(axis == d, coordinate, me[d]) for d in range(3)}

    other = {"col": 1 - core}

    def cs_of(j):
        return pl.ds(pl.multiple_of(j * LANE, LANE), LANE)

    def loop(n, body):
        def step(j, _):
            body(j)
            return 0

        lax.fori_loop(0, n, step, 0)

    def exchange(ref, d, send, recv):
        for step in (1, 2, 3):
            pltpu.make_async_remote_copy(
                ref.at[me[d]], ref.at[me[d]], send, recv,
                device_id={TOK[d]: lax.rem(me[d] + step, 4)}, device_id_type=MESH,
            ).start()

    def exchanged(ref, d, send, recv):
        three = ref.at[pl.ds(0, 3)]
        return pltpu.make_async_remote_copy(
            three, three, send, recv, device_id={TOK[d]: lax.rem(me[d] + 1, 4)}, device_id_type=MESH
        )

    def ring(d):
        return rings.at[d], d, ring_send.at[d], ring_recv.at[d]

    def stat(kind, d):
        return stats.at[kind, d], d, stat_send.at[kind, d], stat_recv.at[kind, d]

    def added(ref):
        return ref[0] + ref[1] + ref[2] + ref[3]

    def stat_next(kind, d):
        now = ring(0) if (kind, d) == (0, 0) else stat(kind, d)
        exchanged(*now).wait_recv()
        stats[kind, d + 1, me[d + 1]] = added(now[0])
        exchange(*stat(kind, d + 1))

    mine = pl.ds(core * half_blocks, half_blocks)
    groups = LANE // block

    def push(lanes, k, half=mine):
        return pltpu.make_async_remote_copy(
            left.at[half, :, lanes], left.at[half, :, lanes], peer_send.at[k], peer_recv.at[k],
            device_id=other, device_id_type=MESH,
        )

    main_push = push(pl.ds(0, depth), 0)
    late_push = push(pl.ds(depth, AUX), 1)
    spread_push = pltpu.make_async_remote_copy(
        spread_first.at[core], spread_first.at[core], peer_send.at[2], peer_recv.at[2],
        device_id=other, device_id_type=MESH,
    )

    count = [counts_ref[w].astype(jnp.float32) for w in range(4)]
    device_count = count[0] + count[1] + count[2] + count[3]
    row16 = lax.broadcasted_iota(jnp.int32, (16, LANE), 0)

    def packed(values, weighted):
        result = jnp.zeros((16, LANE), jnp.float32)
        for w, value in enumerate(values):
            high = value.astype(jnp.bfloat16).astype(jnp.float32)
            low = value - high
            order = (high, high, low, low) if weighted else (high, low, high, low)
            for k in range(4):
                result = jnp.where(row16 == 4 * k + w, order[k], result)
        return result

    def put_left(j, lanes, rows):
        turned = rows.T.astype(jnp.bfloat16)
        for k in range(groups):
            left[core * half_blocks + j * groups + k, :, lanes] = turned[k * block : (k + 1) * block]

    def filled(rows):
        return jnp.concatenate([rows, jnp.zeros((AUX - rows.shape[0], LANE), jnp.float32)], axis=0)

    def prepare(raw):
        loads = []
        for w in range(4):
            lines = pl.ds(w * slots, slots)
            loads.append(pltpu.make_async_copy(first_hbm.at[lines], raw.at[lines], load_sem.at[0, w]))
        for w in range(4):
            lines = pl.ds(w * slots, slots)
            loads.append(pltpu.make_async_copy(second_hbm.at[lines], right.at[lines], load_sem.at[1, w]))
        for copy in loads:
            copy.start()
        barrier = pltpu.get_barrier_semaphore()
        for d in range(3):
            for step in (1, 2, 3):
                pl.semaphore_signal(
                    barrier, inc=1, device_id={TOK[d]: lax.rem(me[d] + step, 4)}, device_id_type=MESH
                )
        pl.semaphore_signal(barrier, inc=1, device_id=other, device_id_type=MESH)

        row = lax.broadcasted_iota(jnp.int32, (8, slots), 0)
        slot = lax.broadcasted_iota(jnp.int32, (8, slots), 1)
        squares[...] = jnp.zeros_like(squares)
        sums_of[...] = jnp.zeros_like(sums_of)

        def total_of(w):
            live = jnp.where((row == w) & (slot < counts_ref[w]), 1.0, 0.0).astype(jnp.bfloat16)
            for which, ref in ((0, raw), (1, right)):
                loads[4 * which + w].wait()
                sums_of[which] += jnp.dot(
                    live, ref[pl.ds(w * slots, slots), :], preferred_element_type=jnp.float32
                )

        def center(w):
            live = lax.broadcasted_iota(jnp.int32, (slots, LANE), 0) < counts_ref[w]
            lines = pl.ds(w * slots, slots)

            def centered_of(ref, which, cs):
                mean = sums_of[which, w : w + 1, cs] / count[w]
                x = jnp.where(live, ref[lines, cs].astype(jnp.float32) - mean, 0.0).astype(jnp.bfloat16)
                wide = x.astype(jnp.float32)
                squares[which, :, cs] += jnp.sum((wide * wide).reshape(slots // 8, 8, LANE), axis=0)
                return x

            def chunk(j):
                cs = cs_of(j)
                turned = centered_of(raw, 0, cs).T
                for k in range(groups):
                    left[core * half_blocks + j * groups + k, :, lines] = turned[k * block : (k + 1) * block]
                right[lines, cs] = centered_of(right, 1, cs)

            loop(width // LANE, chunk)
            push(lines, 0).start()

        total_of(0)
        pl.semaphore_wait(barrier, 10)
        center(0)
        for w in (1, 2):
            total_of(w)
            center(w)
        total_of(3)
        for which in (0, 1):
            device_sum = jnp.sum(sums_of[which], axis=0, keepdims=True)
            for d in range(3):
                rings[d, me[d], which] = device_sum
        for d in range(3):
            rings[d, me[d], 2] = jnp.full((1, width), device_count, jnp.float32)
        for d in range(3):
            exchange(*ring(d))

        def aux_rows(which, cs, weighted):
            device_mean = jnp.sum(sums_of[which, :, cs], axis=0, keepdims=True) / device_count
            values = []
            for w in range(4):
                value = sums_of[which, w : w + 1, cs] / count[w] - device_mean
                values.append(count[w] * value if weighted else value)
            return filled(packed(values, weighted))

        def aux(j):
            cs = cs_of(j)
            put_left(j, pl.ds(tokens, AUX), aux_rows(0, cs, True))
            right[pl.ds(tokens, AUX), cs] = aux_rows(1, cs, False).astype(jnp.bfloat16)

        loop(width // LANE, aux)
        push(pl.ds(tokens, AUX), 0).start()
        center(3)
        main_push.wait_recv()

    def reduce(acc):
        sums = acc.at[3]
        axes = [[lax.rem(core + q + k, 3) for k in range(3)] for q in range(3)]
        here = [[pick(axes[q][k], me) for k in range(3)] for q in range(3)]
        stride = [[pick(axes[q][k], (16, 4, 1)) for k in range(3)] for q in range(3)]

        def columns(q):
            return pl.ds(starts[q], widths[q])

        def moved(q, k, step):
            return lax.rem(here[q][k] + step, 4)

        def device(q, k, step):
            return at(axes[q][k], moved(q, k, step))

        def distance_of(k):
            return pick(k, DISTANCES)

        def multiply(q, first_step, second_step, into=None, lanes=depth):
            into = sums if into is None else into
            base = moved(q, 0, first_step) * stride[q][0] + moved(q, 1, second_step) * stride[q][1]
            deep = pl.ds(0, lanes)
            blocks = [left[base + moved(q, 2, distance) * stride[q][2], :, deep] for distance in DISTANCES]
            into[:, columns(q)] = jnp.dot(
                jnp.concatenate(blocks, axis=0), right[deep, columns(q)], preferred_element_type=jnp.float32
            )

        def multiply_own(q, second_step, into=None):
            multiply(q, 0, second_step, into, depth + AUX)

        def encoded(p, code_ref, scale_ref):
            peak = jnp.maximum(jnp.max(jnp.abs(p), axis=0, keepdims=True), 1e-30)
            code = jnp.round(p * (CODES / peak)).astype(jnp.int32)
            code_ref[...] = code.astype(jnp.int16)
            scale_ref[...] = peak * (1.0 / CODES)

        def encode_sums(q, code_ref, scale_ref):
            for cs in tiles(q):
                encoded(sums[:, cs], code_ref.at[:, cs], scale_ref.at[:, cs])

        def tiles(q):
            return [pl.ds(starts[q] + j, LANE) for j in range(0, widths[q], LANE)]

        def decoded(code_ref, scale_ref):
            return code_ref[...].astype(jnp.int32).astype(jnp.float32) * scale_ref[...]

        def each_tile(q, body):
            def step(j):
                body(pl.ds(pl.multiple_of(starts[q] + j * LANE, LANE), LANE))

            loop(widths[q] // LANE, step)

        def pair(code, code_to, scale, scale_to, sems, q, k, to):
            s, r, t, u = sems
            return (
                pltpu.make_async_remote_copy(
                    code, code_to, s.at[q], r.at[q, k], device_id=to, device_id_type=MESH
                ),
                pltpu.make_async_remote_copy(
                    scale, scale_to, t.at[q], u.at[q, k], device_id=to, device_id_type=MESH
                ),
            )

        far_sems = (far_s, far_r, far_t, far_u)
        near_sems = (near_s, near_r, near_t, near_u)
        mid_sems = (mid_s, mid_r, mid_t, mid_u)
        last_sems = (last_s, last_r, last_t, last_u)

        def far(q, k, way):
            cs = columns(q)
            lines = (upper, lower)[way]
            return pair(
                far_out.at[k, lines, cs], far_in.at[k, lines, cs],
                far_scale.at[k, :, cs], far_scale_in.at[2 * k + way, :, cs],
                far_sems, q, k, device(q, 0, (1, 3)[way]),
            )

        def near(q, n, step):
            cs = columns(q)
            return pair(
                near_out.at[n, :, cs], near_in.at[n, :, cs], near_scale.at[n, :, cs], near_scale_in.at[n, :, cs],
                near_sems, q, n // 2, device(q, 0, step),
            )

        def both(q, k, code, scale, lines, sems, axis):
            cs = columns(q)
            code, scale = code.at[lines[0], :, cs], scale.at[lines[1], :, cs]
            return pair(code, code, scale, scale, sems, q, k, device(q, axis, 1))

        def far_both(q, k):
            return both(q, k, far_in, far_scale_in, (pl.ds(k, 1), pl.ds(2 * k, 2)), far_sems, 0)

        def near_both(q, k):
            return both(q, k, near_in, near_scale_in, (pl.ds(2 * k, 2), pl.ds(2 * k, 2)), near_sems, 0)

        def mid_both(q, k):
            return both(q, k, mid_in, mid_scale_in, ((pl.ds(0, 1), pl.ds(1, 2))[k], pl.ds(2 * k, 2)), mid_sems, 1)

        def last_both(q, k):
            return both(q, k, last_in, last_scale_in, ((pl.ds(0, 1), pl.ds(1, 2))[k], pl.ds(2 * k, 2)), last_sems, 2)

        def far_all(q):
            return both(q, 0, far_in, far_scale_in, (pl.ds(0, 4), pl.ds(0, 8)), far_sems, 0)

        def near_all(q):
            return both(q, 0, near_in, near_scale_in, (pl.ds(0, 8), pl.ds(0, 8)), near_sems, 0)

        def mid_all(q):
            return both(q, 0, mid_in, mid_scale_in, (pl.ds(0, 3), pl.ds(0, 4)), mid_sems, 1)

        def last_all(q):
            return both(q, 0, last_in, last_scale_in, (pl.ds(0, 3), pl.ds(0, 4)), last_sems, 2)

        def start(copies):
            for copy in copies:
                copy.start()

        def arrived(copies):
            for copy in copies:
                copy.wait_recv()

        def gone(copies):
            for copy in copies:
                copy.wait_send()

        def serve_far(k):
            for q in range(3):
                if q < 2:
                    multiply(q + 1, 2, distance_of(k))
                else:
                    multiply(0, jnp.where(k == 3, 1, 2), pick(k, DISTANCES[1:] + DISTANCES[:1]))
                encode_sums(q, far_out.at[k], far_scale.at[k])
                start(far(q, k, 0))
                start(far(q, k, 1))

        def serve_near(k):
            for way in (0, 1):
                n = 2 * k + way
                for q in range(3):
                    if way == 0:
                        arrived(far_both(q, k))
                    if q < 2:
                        multiply(q + 1, (1, 3)[way], distance_of(k))
                    elif way == 0:
                        multiply(0, 3, distance_of(k))
                    else:
                        multiply(0, jnp.where(k == 3, 0, 1), pick(k, DISTANCES[1:] + DISTANCES[3:]))
                    for cs in tiles(q):
                        p = sums[:, cs]
                        more = decoded(far_in.at[k, (upper, lower)[way], cs], far_scale_in.at[n, :, cs])
                        if way == 0:
                            p = jnp.concatenate([p[: rows // 2] + more, p[rows // 2 :]], axis=0)
                        else:
                            p = jnp.concatenate([p[: rows // 2], p[rows // 2 :] + more], axis=0)
                        encoded(p, near_out.at[n, :, cs], near_scale.at[n, :, cs])
                    start(near(q, n, (1, 3)[way]))

        multiply(0, 2, DISTANCES[0])
        stat_next(0, 0)

        def serve_far_all(k):
            serve_far(k)

            @pl.when(k == 1)
            def _():
                stat_next(0, 1)

        loop(4, serve_far_all)

        exchanged(*stat(0, 2)).wait_recv()
        total = added(stats.at[0, 2])
        for which in (0, 1):
            grand[which : which + 1, :] = total[which] / total[2]
        grand_count = total[2, 0, 0]
        for d in (1, 2):
            exchanged(*ring(d)).wait_recv()

        def late_left(j):
            cs = cs_of(j)
            mean = grand[0:1, cs]
            rows = [
                packed([rings[d, m, 0, :, cs] - rings[d, m, 2, :, cs] * mean for m in range(4)], True) for d in range(3)
            ]
            put_left(j, pl.ds(depth, AUX), filled(jnp.concatenate(rows, axis=0)))

        loop(width // LANE, late_left)
        late_push.start()
        for q in range(3):
            d = axes[q][0]

            def late_right(cs):
                mean = grand[1:2, cs]
                rows = packed([rings[d, m, 1, :, cs] / rings[d, m, 2, :, cs] - mean for m in range(4)], False)
                rows = jnp.concatenate([jnp.where(d == k, rows, 0.0) for k in range(3)], axis=0)
                right[pl.ds(depth, AUX), cs] = filled(rows).astype(jnp.bfloat16)

            each_tile(q, late_right)

        eight = lax.broadcasted_iota(jnp.int32, (8, LANE), 0)
        weight_rows = jnp.zeros((8, LANE), jnp.float32)
        for w in range(4):
            weight_rows = jnp.where(eight == w, count[w], weight_rows)
        count_rows = jnp.maximum(weight_rows, 1.0)

        def spread(j):
            cs = cs_of(j)
            for which in (0, 1):
                shift = sums_of[which, :, cs] / count_rows - grand[which : which + 1, cs]
                part = squares[which, :, cs] + weight_rows * shift * shift
                stats[1, 0, me[0], which, :, cs] = jnp.sum(part, axis=0, keepdims=True)

        stats[1, 0, me[0], 2] = jnp.zeros((1, width), jnp.float32)
        loop(width // LANE, spread)
        exchange(*stat(1, 0))

        mid_out = far_out

        def mid(q, n, way=0):
            cs = columns(q)
            lines = (upper, lower)[way] if n == 0 else pl.ds(0, rows)
            k = way if n == 0 else n + 1
            step = (1, 3)[way] if n == 0 else (1, 3)[n - 1]
            return pair(
                mid_out.at[n, lines, cs], mid_in.at[n, lines, cs], mid_scale.at[n, :, cs], mid_scale_in.at[k, :, cs],
                mid_sems, q, k // 2, device(q, 1, step),
            )

        def merged(k, cs):
            n = 2 * k
            return (
                acc[k, :, cs]
                + decoded(near_in.at[n, :, cs], near_scale_in.at[n, :, cs])
                + decoded(near_in.at[n + 1, :, cs], near_scale_in.at[n + 1, :, cs])
            )

        def take_own(k):
            for q in range(3):
                arrived(near_both(q, k))
                if k == 1:
                    arrived(mid_both(q, 0))

                def body(cs):
                    p = merged(k, cs)
                    if k == 3:
                        sums[:, cs] = p
                        return
                    if k == 1:
                        more = decoded(mid_in.at[0, upper, cs], mid_scale_in.at[0, :, cs])
                        p = jnp.concatenate([p[: rows // 2] + more, p[rows // 2 :]], axis=0)
                    if k == 2:
                        more = decoded(mid_in.at[0, lower, cs], mid_scale_in.at[1, :, cs])
                        p = jnp.concatenate([p[: rows // 2], p[rows // 2 :] + more], axis=0)
                    encoded(p, mid_out.at[k, :, cs], mid_scale.at[k, :, cs])

                each_tile(q, body)
                if k == 0:
                    start(mid(q, 0, 0))
                    start(mid(q, 0, 1))
                elif k < 3:
                    start(mid(q, k))

        def serve(k):
            serve_near(k)

            @pl.when(k == 0)
            def _():
                stat_next(1, 0)
                late_push.wait_recv()

            @pl.when(k == 1)
            def _():
                stat_next(1, 1)
                for q in range(3):
                    gone(far_all(q))

            @pl.when(k >= 1)
            def _():
                for q in range(3):
                    multiply_own(q, distance_of(k - 1), acc.at[k - 1])

            for before in range(3):

                @pl.when(k == before + 1)
                def _():
                    take_own(before)

        loop(4, serve)
        for q in range(3):
            multiply_own(q, 0)
        take_own(3)
        exchanged(*stat(1, 2)).wait_recv()
        spread_first[core] = added(stats.at[1, 2])
        spread_push.start()

        part = rows // 4
        half = part // 2
        front, back = pl.ds(0, half), pl.ds(half, half)

        def last(q, n, way=0):
            cs = columns(q)
            lines = (front, back)[way] if n == 0 else pl.ds(0, part)
            k = way if n == 0 else n + 1
            step = (1, 3)[way] if n == 0 else (1, 3)[n - 1]
            return pair(
                last_out.at[n, lines, cs], last_in.at[n, lines, cs], last_scale.at[n, :, cs], last_scale_in.at[k, :, cs],
                last_sems, q, k // 2, device(q, 2, step),
            )

        for q in range(3):
            arrived(mid_both(q, 1))

            def body(cs):
                p = (
                    sums[:, cs]
                    + decoded(mid_in.at[1, :, cs], mid_scale_in.at[2, :, cs])
                    + decoded(mid_in.at[2, :, cs], mid_scale_in.at[3, :, cs])
                )
                encoded(p[:part], last_out.at[0, :, cs], last_scale.at[0, :, cs])
                sums[pl.ds(part, 3 * part), cs] = p[part:]

            each_tile(q, body)
            start(last(q, 0, 0))
            start(last(q, 0, 1))

        for q in range(3):
            arrived(last_both(q, 0))

            def body(cs):
                ahead = jnp.concatenate(
                    [
                        sums[pl.ds(part, half), cs] + decoded(last_in.at[0, front, cs], last_scale_in.at[0, :, cs]),
                        sums[pl.ds(part + half, half), cs],
                    ],
                    axis=0,
                )
                encoded(ahead, last_out.at[1, :, cs], last_scale.at[1, :, cs])
                behind = jnp.concatenate(
                    [
                        sums[pl.ds(2 * part, half), cs],
                        sums[pl.ds(2 * part + half, half), cs]
                        + decoded(last_in.at[0, back, cs], last_scale_in.at[1, :, cs]),
                    ],
                    axis=0,
                )
                encoded(behind, last_out.at[2, :, cs], last_scale.at[2, :, cs])

            each_tile(q, body)
            start(last(q, 1))
            start(last(q, 2))

        spread_push.wait_recv()
        row_block = me[0] * 16 + me[1] * 4 + me[2]
        in_half = lax.rem(row_block, half_blocks)
        lane_block = cs_of(in_half * block // LANE)
        line = spread_first[row_block // half_blocks, 0, :, lane_block] / grand_count
        column[...] = jnp.broadcast_to(line, (LANE, LANE)).T
        rows_var = column[pl.ds(pl.multiple_of(lax.rem(in_half, groups) * block, block), block), :] + 0.1

        for q in range(3):
            arrived(last_both(q, 1))

            def body(cs):
                cross = (
                    sums[pl.ds(3 * part, part), cs]
                    + decoded(last_in.at[1, :, cs], last_scale_in.at[2, :, cs])
                    + decoded(last_in.at[2, :, cs], last_scale_in.at[3, :, cs])
                )
                columns_var = spread_first[core, 1, :, cs] / grand_count + 0.1
                out_ref[pl.ds(0, block), cs] = cross / grand_count * lax.rsqrt(rows_var * columns_var)

            each_tile(q, body)

        out_ref[pl.ds(block, 2), :] = grand[0:2, :]

        for q in range(3):
            for copies in (near_all(q), mid_all(q), last_all(q)):
                gone(copies)
        for copy in (main_push, late_push, spread_push):
            copy.wait_send()
        for d in range(3):
            exchanged(*ring(d)).wait_send()
            exchanged(*stat(1, d)).wait_send()
            if d > 0:
                exchanged(*stat(0, d)).wait_send()

    pl.run_scoped(prepare, pltpu.VMEM((tokens, width), jnp.bfloat16))
    pl.run_scoped(reduce, pltpu.VMEM((4, rows, width), jnp.float32))


def local(first_acts, second_acts, window_counts):
    tokens, width = first_acts.shape
    block = width * lax.axis_size("col") // lax.axis_size(TOK)
    blocks = width // block
    rows, depth = 4 * block, tokens + 2 * AUX
    i16, f32, bf16 = jnp.int16, jnp.float32, jnp.bfloat16
    dma = pltpu.SemaphoreType.DMA
    vmem = pltpu.VMEM
    out = pl.pallas_call(
        functools.partial(kernel, widths_of(width)),
        out_shape=jax.ShapeDtypeStruct((block + 8, width), f32),
        in_specs=[
            pl.BlockSpec(memory_space=pltpu.SMEM),
            pl.BlockSpec(memory_space=pl.ANY),
            pl.BlockSpec(memory_space=pl.ANY),
        ],
        out_specs=pl.BlockSpec(memory_space=vmem),
        scratch_shapes=[
            vmem((2 * blocks, block, depth), bf16),
            vmem((depth, width), bf16),
            vmem((4, rows, width), i16), vmem((4, rows, width), i16),
            vmem((8, rows, width), i16), vmem((8, rows, width), i16),
            vmem((3, block, width), i16), vmem((3, block, width), i16),
            vmem((3, rows, width), i16),
            vmem((4, 1, width), f32), vmem((8, 1, width), f32),
            vmem((8, 1, width), f32), vmem((8, 1, width), f32),
            vmem((3, 1, width), f32), vmem((4, 1, width), f32),
            vmem((3, 1, width), f32), vmem((4, 1, width), f32),
            vmem((2, 8, width), f32), vmem((2, 8, width), f32),
            vmem((3, 4, 3, 1, width), f32),
            vmem((2, 3, 4, 3, 1, width), f32),
            vmem((2, 3, 1, width), f32),
            vmem((8, width), f32),
            vmem((LANE, LANE), f32),
            dma((2, 4)), dma((3,)), dma((3,)),
            dma((3,)), dma((3,)), dma((2, 3)), dma((2, 3)),
            dma((3,)), dma((3, 4)), dma((3,)), dma((3, 4)),
            dma((3,)), dma((3, 4)), dma((3,)), dma((3, 4)),
            dma((3,)), dma((3, 2)), dma((3,)), dma((3, 2)),
            dma((3,)), dma((3, 2)), dma((3,)), dma((3, 2)),
        ],
        compiler_params=pltpu.CompilerParams(
            collective_id=0, has_side_effects=True, vmem_limit_bytes=67_043_328
        ),
        cost_estimate=pl.CostEstimate(
            flops=4 * width * width * depth, bytes_accessed=30_000_000, transcendentals=0
        ),
        name="whole",
    )(window_counts, first_acts, second_acts)
    return out[:block], out[block : block + 2]


def solution(mesh):
    torus = Mesh(
        mesh.devices.reshape(4, 4, 4, mesh.shape["col"]), ("tok_0", "tok_1", "tok_2", "col")
    )
    return jax.shard_map(
        local,
        mesh=torus,
        in_specs=(P(TOK, "col"), P(TOK, "col"), P(TOK)),
        out_specs=(P(TOK, "col"), P(None, "col")),
        check_vma=False,
    )
```

time: 112 us -> 111 us (level); the launches traced: 110 us -> 111 us
    slice x0 -> x2, local copies, waits for them, and re-layouts: none -> 3.32 us  [local(): return (out[:block], out[block:block + 2])]
    unnamed x2 -> x0, local copies, waits for them, and re-layouts: 3.2 us -> none
where the time goes in v4:
time: 111 us
  Pallas kernels  107 us (96%)
  local copies, waits for them, and re-layouts  3.32 us (3%)
    pallas_call x1, Pallas kernels, local(): pl.pallas_call(functools.partial(kernel, widths_of(width)), out_shape=jax...  107 us
    slice x2, local copies, waits for them, and re-layouts, local(): return (out[:block], out[block:block + 2])  3.32 us

profile of v4, /device:TPU:0, one launch (start us, length us, event | category | flops | bytes accessed | tf_op | source)
XLA Modules:
  0.0 111.2 jit_solution(7601058284442599341)
XLA Ops:
  0.6 107.3 %whole.1 = f32[72,2048]{1,0:T(8,128)} custom-call(s32[4]{0:T(128)} %counts_ref.1, bf16[1536,2048]{1,0:T(8,128)(2,1)} %first_hbm.1, bf16[1536,2048]{1,0:T(8,128)(2,1)} %second_hbm.1), custom_call_target="tpu_custom_call" | custom-call | flops 30064771072 | bytes 30000000 | tf_op jit(solution)/shard_map/whole/pallas_call | solution.py:618
  107.9 1.4 %slice.7 = f32[2,2048]{1,0:T(2,128)} slice(f32[72,2048]{1,0:T(8,128)} %whole.1), slice={[64:66], [0:2048]} | slice | bytes 32768 | tf_op jit(solution)/shard_map/slice | solution.py:659
  109.3 1.9 %slice.6 = f32[64,2048]{1,0:T(8,128)} slice(f32[72,2048]{1,0:T(8,128)} %whole.1), slice={[0:64], [0:2048]} | slice | bytes 1048576 | tf_op jit(solution)/shard_map/slice | solution.py:659

commit v5 on v4

--- a/solution.py
+++ b/solution.py
@@ -66,6 +66,13 @@
 
         lax.fori_loop(0, n, step, 0)
 
+    def loop_by(n, unroll, body):
+        def step(j):
+            for i in range(unroll):
+                body(j * unroll + i)
+
+        loop(n // unroll, step)
+
     def exchange(ref, d, send, recv):
         for step in (1, 2, 3):
             pltpu.make_async_remote_copy(
@@ -137,8 +144,6 @@
         for w in range(4):
             lines = pl.ds(w * slots, slots)
             loads.append(pltpu.make_async_copy(first_hbm.at[lines], raw.at[lines], load_sem.at[0, w]))
-        for w in range(4):
-            lines = pl.ds(w * slots, slots)
             loads.append(pltpu.make_async_copy(second_hbm.at[lines], right.at[lines], load_sem.at[1, w]))
         for copy in loads:
             copy.start()
@@ -158,7 +163,7 @@
         def total_of(w):
             live = jnp.where((row == w) & (slot < counts_ref[w]), 1.0, 0.0).astype(jnp.bfloat16)
             for which, ref in ((0, raw), (1, right)):
-                loads[4 * which + w].wait()
+                loads[2 * w + which].wait()
                 sums_of[which] += jnp.dot(
                     live, ref[pl.ds(w * slots, slots), :], preferred_element_type=jnp.float32
                 )
@@ -181,11 +186,15 @@
                     left[core * half_blocks + j * groups + k, :, lines] = turned[k * block : (k + 1) * block]
                 right[lines, cs] = centered_of(right, 1, cs)
 
-            loop(width // LANE, chunk)
-            push(lines, 0).start()
+            pieces = 4 if w == 3 else 1
+            chunks, step = width // LANE // pieces, half_blocks // pieces
+            for piece in range(pieces):
+                loop_by(chunks, 2, lambda j: chunk(piece * chunks + j))
+                if w == 0:
+                    pl.semaphore_wait(barrier, 10)
+                push(lines, 0, pl.ds(core * half_blocks + piece * step, step)).start()
 
         total_of(0)
-        pl.semaphore_wait(barrier, 10)
         center(0)
         for w in (1, 2):
             total_of(w)
@@ -213,7 +222,7 @@
             put_left(j, pl.ds(tokens, AUX), aux_rows(0, cs, True))
             right[pl.ds(tokens, AUX), cs] = aux_rows(1, cs, False).astype(jnp.bfloat16)
 
-        loop(width // LANE, aux)
+        loop_by(width // LANE, 4, aux)
         push(pl.ds(tokens, AUX), 0).start()
         center(3)
         main_push.wait_recv()
@@ -350,15 +359,17 @@
                 else:
                     multiply(0, jnp.where(k == 3, 1, 2), pick(k, DISTANCES[1:] + DISTANCES[:1]))
                 encode_sums(q, far_out.at[k], far_scale.at[k])
+            for q in range(3):
                 start(far(q, k, 0))
                 start(far(q, k, 1))
 
         def serve_near(k):
             for way in (0, 1):
                 n = 2 * k + way
+                if way == 0:
+                    for q in range(3):
+                        arrived(far_both(q, k))
                 for q in range(3):
-                    if way == 0:
-                        arrived(far_both(q, k))
                     if q < 2:
                         multiply(q + 1, (1, 3)[way], distance_of(k))
                     elif way == 0:
@@ -373,6 +384,7 @@
                         else:
                             p = jnp.concatenate([p[: rows // 2], p[rows // 2 :] + more], axis=0)
                         encoded(p, near_out.at[n, :, cs], near_scale.at[n, :, cs])
+                for q in range(3):
                     start(near(q, n, (1, 3)[way]))
 
         multiply(0, 2, DISTANCES[0])
@@ -387,51 +399,51 @@
 
         loop(4, serve_far_all)
 
-        exchanged(*stat(0, 2)).wait_recv()
-        total = added(stats.at[0, 2])
-        for which in (0, 1):
-            grand[which : which + 1, :] = total[which] / total[2]
-        grand_count = total[2, 0, 0]
-        for d in (1, 2):
-            exchanged(*ring(d)).wait_recv()
-
-        def late_left(j):
-            cs = cs_of(j)
-            mean = grand[0:1, cs]
-            rows = [
-                packed([rings[d, m, 0, :, cs] - rings[d, m, 2, :, cs] * mean for m in range(4)], True) for d in range(3)
-            ]
-            put_left(j, pl.ds(depth, AUX), filled(jnp.concatenate(rows, axis=0)))
-
-        loop(width // LANE, late_left)
-        late_push.start()
-        for q in range(3):
-            d = axes[q][0]
-
-            def late_right(cs):
-                mean = grand[1:2, cs]
-                rows = packed([rings[d, m, 1, :, cs] / rings[d, m, 2, :, cs] - mean for m in range(4)], False)
-                rows = jnp.concatenate([jnp.where(d == k, rows, 0.0) for k in range(3)], axis=0)
-                right[pl.ds(depth, AUX), cs] = filled(rows).astype(jnp.bfloat16)
-
-            each_tile(q, late_right)
-
-        eight = lax.broadcasted_iota(jnp.int32, (8, LANE), 0)
-        weight_rows = jnp.zeros((8, LANE), jnp.float32)
-        for w in range(4):
-            weight_rows = jnp.where(eight == w, count[w], weight_rows)
-        count_rows = jnp.maximum(weight_rows, 1.0)
-
-        def spread(j):
-            cs = cs_of(j)
+        def take_grand():
+            exchanged(*stat(0, 2)).wait_recv()
+            total = added(stats.at[0, 2])
             for which in (0, 1):
-                shift = sums_of[which, :, cs] / count_rows - grand[which : which + 1, cs]
-                part = squares[which, :, cs] + weight_rows * shift * shift
-                stats[1, 0, me[0], which, :, cs] = jnp.sum(part, axis=0, keepdims=True)
-
-        stats[1, 0, me[0], 2] = jnp.zeros((1, width), jnp.float32)
-        loop(width // LANE, spread)
-        exchange(*stat(1, 0))
+                grand[which : which + 1, :] = total[which] / total[2]
+            for d in (1, 2):
+                exchanged(*ring(d)).wait_recv()
+
+            def late_left(j):
+                cs = cs_of(j)
+                mean = grand[0:1, cs]
+                rows = [
+                    packed([rings[d, m, 0, :, cs] - rings[d, m, 2, :, cs] * mean for m in range(4)], True) for d in range(3)
+                ]
+                put_left(j, pl.ds(depth, AUX), filled(jnp.concatenate(rows, axis=0)))
+
+            loop_by(width // LANE, 4, late_left)
+            late_push.start()
+            for q in range(3):
+                d = axes[q][0]
+
+                def late_right(cs):
+                    mean = grand[1:2, cs]
+                    rows = packed([rings[d, m, 1, :, cs] / rings[d, m, 2, :, cs] - mean for m in range(4)], False)
+                    rows = jnp.concatenate([jnp.where(d == k, rows, 0.0) for k in range(3)], axis=0)
+                    right[pl.ds(depth, AUX), cs] = filled(rows).astype(jnp.bfloat16)
+
+                each_tile(q, late_right)
+
+            eight = lax.broadcasted_iota(jnp.int32, (8, LANE), 0)
+            weight_rows = jnp.zeros((8, LANE), jnp.float32)
+            for w in range(4):
+                weight_rows = jnp.where(eight == w, count[w], weight_rows)
+            count_rows = jnp.maximum(weight_rows, 1.0)
+
+            def spread(j):
+                cs = cs_of(j)
+                for which in (0, 1):
+                    shift = sums_of[which, :, cs] / count_rows - grand[which : which + 1, cs]
+                    part = squares[which, :, cs] + weight_rows * shift * shift
+                    stats[1, 0, me[0], which, :, cs] = jnp.sum(part, axis=0, keepdims=True)
+
+            stats[1, 0, me[0], 2] = jnp.zeros((1, width), jnp.float32)
+            loop(width // LANE, spread)
+            exchange(*stat(1, 0))
 
         mid_out = far_out
 
@@ -453,8 +465,8 @@
                 + decoded(near_in.at[n + 1, :, cs], near_scale_in.at[n + 1, :, cs])
             )
 
-        def take_own(k):
-            for q in range(3):
+        def take_own(k, groups_of=(0, 1, 2)):
+            for q in groups_of:
                 arrived(near_both(q, k))
                 if k == 1:
                     arrived(mid_both(q, 0))
@@ -484,14 +496,17 @@
 
             @pl.when(k == 0)
             def _():
-                stat_next(1, 0)
-                late_push.wait_recv()
+                take_grand()
 
             @pl.when(k == 1)
             def _():
-                stat_next(1, 1)
+                late_push.wait_recv()
                 for q in range(3):
                     gone(far_all(q))
+
+            @pl.when(k == 2)
+            def _():
+                stat_next(1, 0)
 
             @pl.when(k >= 1)
             def _():
@@ -505,12 +520,9 @@
                     take_own(before)
 
         loop(4, serve)
+        stat_next(1, 1)
         for q in range(3):
             multiply_own(q, 0)
-        take_own(3)
-        exchanged(*stat(1, 2)).wait_recv()
-        spread_first[core] = added(stats.at[1, 2])
-        spread_push.start()
 
         part = rows // 4
         half = part // 2
@@ -527,6 +539,7 @@
             )
 
         for q in range(3):
+            take_own(3, (q,))
             arrived(mid_both(q, 1))
 
             def body(cs):
@@ -542,6 +555,9 @@
             start(last(q, 0, 0))
             start(last(q, 0, 1))
 
+        exchanged(*stat(1, 2)).wait_recv()
+        spread_first[core] = added(stats.at[1, 2])
+        spread_push.start()
         for q in range(3):
             arrived(last_both(q, 0))
 
@@ -569,6 +585,7 @@
             start(last(q, 2))
 
         spread_push.wait_recv()
+        grand_count = added(stats.at[0, 2])[2, 0, 0]
         row_block = me[0] * 16 + me[1] * 4 + me[2]
         in_half = lax.rem(row_block, half_blocks)
         lane_block = cs_of(in_half * block // LANE)

time: 111 us -> 104 us (0.937)
  Pallas kernels: 107 us -> 99.3 us
    pallas_call x1, Pallas kernels: 107 us -> 99.3 us  [local(): pl.pallas_call(functools.partial(kernel, widths_of(width)), out_shape=jax...]
where the time goes in v5:
time: 104 us; the launch traced here: 103 us
  Pallas kernels  99.3 us (95%)
  local copies, waits for them, and re-layouts  3.32 us (3%)
    pallas_call x1, Pallas kernels, local(): pl.pallas_call(functools.partial(kernel, widths_of(width)), out_shape=jax...  99.3 us
    slice x2, local copies, waits for them, and re-layouts, local(): return (out[:block], out[block:block + 2])  3.32 us

profile of v5, /device:TPU:0, one launch (start us, length us, event | category | flops | bytes accessed | tf_op | source)
XLA Modules:
  0.0 103.3 jit_solution(10694623755368251664)
XLA Ops:
  0.6 99.3 %whole.1 = f32[72,2048]{1,0:T(8,128)} custom-call(s32[4]{0:T(128)} %counts_ref.1, bf16[1536,2048]{1,0:T(8,128)(2,1)} %first_hbm.1, bf16[1536,2048]{1,0:T(8,128)(2,1)} %second_hbm.1), custom_call_target="tpu_custom_call" | custom-call | flops 30064771072 | bytes 30000000 | tf_op jit(solution)/shard_map/whole/pallas_call | solution.py:635
  100.0 1.4 %slice.7 = f32[2,2048]{1,0:T(2,128)} slice(f32[72,2048]{1,0:T(8,128)} %whole.1), slice={[64:66], [0:2048]} | slice | bytes 32768 | tf_op jit(solution)/shard_map/slice | solution.py:676
  101.4 1.9 %slice.6 = f32[64,2048]{1,0:T(8,128)} slice(f32[72,2048]{1,0:T(8,128)} %whole.1), slice={[0:64], [0:2048]} | slice | bytes 1048576 | tf_op jit(solution)/shard_map/slice | solution.py:676

commit v6 on v5

--- a/solution.py
+++ b/solution.py
@@ -34,7 +34,7 @@
     counts_ref, first_hbm, second_hbm, out_ref,
     left, right, far_out, far_in, near_out, near_in, last_out, last_in, mid_in,
     far_scale, far_scale_in, near_scale, near_scale_in, mid_scale, mid_scale_in, last_scale, last_scale_in,
-    sums_of, squares, rings, stats, spread_first, grand, column,
+    sums_of, squares, live_slots, rings, stats, spread_first, grand, column,
     load_sem, peer_send, peer_recv, ring_send, ring_recv, stat_send, stat_recv,
     far_s, far_r, far_t, far_u, near_s, near_r, near_t, near_u,
     mid_s, mid_r, mid_t, mid_u, last_s, last_r, last_t, last_u,
@@ -56,6 +56,8 @@
 
     other = {"col": 1 - core}
 
+    tail = pl.ds(width, LANE)
+
     def cs_of(j):
         return pl.ds(pl.multiple_of(j * LANE, LANE), LANE)
 
@@ -170,11 +172,12 @@
 
         def center(w):
             live = lax.broadcasted_iota(jnp.int32, (slots, LANE), 0) < counts_ref[w]
+            live_slots[...] = jnp.where(live, 1.0, 0.0).astype(jnp.bfloat16)
             lines = pl.ds(w * slots, slots)
 
             def centered_of(ref, which, cs):
                 mean = sums_of[which, w : w + 1, cs] / count[w]
-                x = jnp.where(live, ref[lines, cs].astype(jnp.float32) - mean, 0.0).astype(jnp.bfloat16)
+                x = (ref[lines, cs].astype(jnp.float32) - mean).astype(jnp.bfloat16) * live_slots[...]
                 wide = x.astype(jnp.float32)
                 squares[which, :, cs] += jnp.sum((wide * wide).reshape(slots // 8, 8, LANE), axis=0)
                 return x
@@ -186,7 +189,7 @@
                     left[core * half_blocks + j * groups + k, :, lines] = turned[k * block : (k + 1) * block]
                 right[lines, cs] = centered_of(right, 1, cs)
 
-            pieces = 4 if w == 3 else 1
+            pieces = (1, 2, 2, 4)[w]
             chunks, step = width // LANE // pieces, half_blocks // pieces
             for piece in range(pieces):
                 loop_by(chunks, 2, lambda j: chunk(piece * chunks + j))
@@ -203,9 +206,8 @@
         for which in (0, 1):
             device_sum = jnp.sum(sums_of[which], axis=0, keepdims=True)
             for d in range(3):
-                rings[d, me[d], which] = device_sum
-        for d in range(3):
-            rings[d, me[d], 2] = jnp.full((1, width), device_count, jnp.float32)
+                rings[d, me[d], which, :, pl.ds(0, width)] = device_sum
+                rings[d, me[d], which, :, tail] = jnp.full((1, LANE), device_count, jnp.float32)
         for d in range(3):
             exchange(*ring(d))
 
@@ -283,10 +285,10 @@
             s, r, t, u = sems
             return (
                 pltpu.make_async_remote_copy(
-                    code, code_to, s.at[q], r.at[q, k], device_id=to, device_id_type=MESH
+                    code, code_to, s.at[0], r.at[q, k], device_id=to, device_id_type=MESH
                 ),
                 pltpu.make_async_remote_copy(
-                    scale, scale_to, t.at[q], u.at[q, k], device_id=to, device_id_type=MESH
+                    scale, scale_to, t.at[0], u.at[q, k], device_id=to, device_id_type=MESH
                 ),
             )
 
@@ -301,7 +303,7 @@
             return pair(
                 far_out.at[k, lines, cs], far_in.at[k, lines, cs],
                 far_scale.at[k, :, cs], far_scale_in.at[2 * k + way, :, cs],
-                far_sems, q, k, device(q, 0, (1, 3)[way]),
+                far_sems, 0, k, device(q, 0, (1, 3)[way]),
             )
 
         def near(q, n, step):
@@ -312,12 +314,13 @@
             )
 
         def both(q, k, code, scale, lines, sems, axis):
-            cs = columns(q)
+            cs = pl.ds(0, width) if q is None else columns(q)
+            q = 0 if q is None else q
             code, scale = code.at[lines[0], :, cs], scale.at[lines[1], :, cs]
             return pair(code, code, scale, scale, sems, q, k, device(q, axis, 1))
 
-        def far_both(q, k):
-            return both(q, k, far_in, far_scale_in, (pl.ds(k, 1), pl.ds(2 * k, 2)), far_sems, 0)
+        def far_both(k):
+            return both(None, k, far_in, far_scale_in, (pl.ds(k, 1), pl.ds(2 * k, 2)), far_sems, 0)
 
         def near_both(q, k):
             return both(q, k, near_in, near_scale_in, (pl.ds(2 * k, 2), pl.ds(2 * k, 2)), near_sems, 0)
@@ -326,19 +329,19 @@
             return both(q, k, mid_in, mid_scale_in, ((pl.ds(0, 1), pl.ds(1, 2))[k], pl.ds(2 * k, 2)), mid_sems, 1)
 
         def last_both(q, k):
-            return both(q, k, last_in, last_scale_in, ((pl.ds(0, 1), pl.ds(1, 2))[k], pl.ds(2 * k, 2)), last_sems, 2)
-
-        def far_all(q):
-            return both(q, 0, far_in, far_scale_in, (pl.ds(0, 4), pl.ds(0, 8)), far_sems, 0)
-
-        def near_all(q):
-            return both(q, 0, near_in, near_scale_in, (pl.ds(0, 8), pl.ds(0, 8)), near_sems, 0)
-
-        def mid_all(q):
-            return both(q, 0, mid_in, mid_scale_in, (pl.ds(0, 3), pl.ds(0, 4)), mid_sems, 1)
-
-        def last_all(q):
-            return both(q, 0, last_in, last_scale_in, (pl.ds(0, 3), pl.ds(0, 4)), last_sems, 2)
+            return both(q, k, last_in, last_scale_in, ((pl.ds(0, 1), pl.ds(1, 2))[k], (pl.ds(0, 2), pl.ds(2, 4))[k]), last_sems, 2)
+
+        def far_all():
+            return both(None, 0, far_in, far_scale_in, (pl.ds(0, 4), pl.ds(0, 8)), far_sems, 0)
+
+        def near_all():
+            return both(None, 0, near_in, near_scale_in, (pl.ds(0, 8), pl.ds(0, 8)), near_sems, 0)
+
+        def mid_all():
+            return both(None, 0, mid_in, mid_scale_in, (pl.ds(0, 3), pl.ds(0, 4)), mid_sems, 1)
+
+        def last_all():
+            return both(None, 0, last_in, last_scale_in, (pl.ds(0, 3), pl.ds(0, 6)), last_sems, 2)
 
         def start(copies):
             for copy in copies:
@@ -367,8 +370,7 @@
             for way in (0, 1):
                 n = 2 * k + way
                 if way == 0:
-                    for q in range(3):
-                        arrived(far_both(q, k))
+                    arrived(far_both(k))
                 for q in range(3):
                     if q < 2:
                         multiply(q + 1, (1, 3)[way], distance_of(k))
@@ -388,22 +390,30 @@
                     start(near(q, n, (1, 3)[way]))
 
         multiply(0, 2, DISTANCES[0])
+        for q in range(3):
+            if q < 2:
+                multiply(q + 1, 2, DISTANCES[0])
+            else:
+                multiply(0, 2, DISTANCES[1])
+            encode_sums(q, far_out.at[0], far_scale.at[0])
+            start(far(q, 0, 0))
+            start(far(q, 0, 1))
         stat_next(0, 0)
 
         def serve_far_all(k):
             serve_far(k)
 
-            @pl.when(k == 1)
+            @pl.when(k == 3)
             def _():
                 stat_next(0, 1)
 
-        loop(4, serve_far_all)
+        loop(3, lambda k: serve_far_all(k + 1))
 
         def take_grand():
             exchanged(*stat(0, 2)).wait_recv()
             total = added(stats.at[0, 2])
             for which in (0, 1):
-                grand[which : which + 1, :] = total[which] / total[2]
+                grand[which : which + 1, :] = total[which, :, :width] / total[which, 0, width]
             for d in (1, 2):
                 exchanged(*ring(d)).wait_recv()
 
@@ -411,7 +421,7 @@
                 cs = cs_of(j)
                 mean = grand[0:1, cs]
                 rows = [
-                    packed([rings[d, m, 0, :, cs] - rings[d, m, 2, :, cs] * mean for m in range(4)], True) for d in range(3)
+                    packed([rings[d, m, 0, :, cs] - rings[d, m, 0, :, tail] * mean for m in range(4)], True) for d in range(3)
                 ]
                 put_left(j, pl.ds(depth, AUX), filled(jnp.concatenate(rows, axis=0)))
 
@@ -422,7 +432,7 @@
 
                 def late_right(cs):
                     mean = grand[1:2, cs]
-                    rows = packed([rings[d, m, 1, :, cs] / rings[d, m, 2, :, cs] - mean for m in range(4)], False)
+                    rows = packed([rings[d, m, 1, :, cs] / rings[d, m, 1, :, tail] - mean for m in range(4)], False)
                     rows = jnp.concatenate([jnp.where(d == k, rows, 0.0) for k in range(3)], axis=0)
                     right[pl.ds(depth, AUX), cs] = filled(rows).astype(jnp.bfloat16)
 
@@ -441,7 +451,8 @@
                     part = squares[which, :, cs] + weight_rows * shift * shift
                     stats[1, 0, me[0], which, :, cs] = jnp.sum(part, axis=0, keepdims=True)
 
-            stats[1, 0, me[0], 2] = jnp.zeros((1, width), jnp.float32)
+            for which in (0, 1):
+                stats[1, 0, me[0], which, :, tail] = jnp.zeros((1, LANE), jnp.float32)
             loop(width // LANE, spread)
             exchange(*stat(1, 0))
 
@@ -494,49 +505,54 @@
         def serve(k):
             serve_near(k)
 
-            @pl.when(k == 0)
+            @pl.when(k == 1)
             def _():
                 take_grand()
-
-            @pl.when(k == 1)
+                gone(far_all())
+
+            @pl.when(k == 2)
             def _():
                 late_push.wait_recv()
+
+            @pl.when(k >= 2)
+            def _():
                 for q in range(3):
-                    gone(far_all(q))
-
-            @pl.when(k == 2)
+                    multiply_own(q, distance_of(k - 2), acc.at[k - 2])
+
+            for before in range(2):
+
+                @pl.when(k == before + 2)
+                def _():
+                    take_own(before)
+
+            @pl.when(k == 3)
             def _():
                 stat_next(1, 0)
-
-            @pl.when(k >= 1)
-            def _():
                 for q in range(3):
-                    multiply_own(q, distance_of(k - 1), acc.at[k - 1])
-
-            for before in range(3):
-
-                @pl.when(k == before + 1)
-                def _():
-                    take_own(before)
+                    multiply_own(q, DISTANCES[2], acc.at[2])
 
         loop(4, serve)
-        stat_next(1, 1)
+        take_own(2)
         for q in range(3):
             multiply_own(q, 0)
+        stat_next(1, 1)
 
         part = rows // 4
         half = part // 2
         front, back = pl.ds(0, half), pl.ds(half, half)
 
-        def last(q, n, way=0):
+        def last(q, n, way):
             cs = columns(q)
-            lines = (front, back)[way] if n == 0 else pl.ds(0, part)
-            k = way if n == 0 else n + 1
+            lines = (front, back)[way]
             step = (1, 3)[way] if n == 0 else (1, 3)[n - 1]
             return pair(
-                last_out.at[n, lines, cs], last_in.at[n, lines, cs], last_scale.at[n, :, cs], last_scale_in.at[k, :, cs],
-                last_sems, q, k // 2, device(q, 2, step),
+                last_out.at[n, lines, cs], last_in.at[n, lines, cs],
+                last_scale.at[2 * n + way, :, cs], last_scale_in.at[2 * n + way, :, cs],
+                last_sems, q, min(n, 1), device(q, 2, step),
             )
+
+        def put_last(p, n, way, cs):
+            encoded(p, last_out.at[n, (front, back)[way], cs], last_scale.at[2 * n + way, :, cs])
 
         for q in range(3):
             take_own(3, (q,))
@@ -548,44 +564,36 @@
                     + decoded(mid_in.at[1, :, cs], mid_scale_in.at[2, :, cs])
                     + decoded(mid_in.at[2, :, cs], mid_scale_in.at[3, :, cs])
                 )
-                encoded(p[:part], last_out.at[0, :, cs], last_scale.at[0, :, cs])
+                put_last(p[:half], 0, 0, cs)
+                put_last(p[half:part], 0, 1, cs)
+                put_last(p[part + half : 2 * part], 1, 1, cs)
+                put_last(p[2 * part : 2 * part + half], 2, 0, cs)
                 sums[pl.ds(part, 3 * part), cs] = p[part:]
 
             each_tile(q, body)
-            start(last(q, 0, 0))
-            start(last(q, 0, 1))
+            for n, way in ((0, 0), (0, 1), (1, 1), (2, 0)):
+                start(last(q, n, way))
+
+        for q in range(3):
+            arrived(last_both(q, 0))
+
+            def body(cs):
+                ahead = sums[pl.ds(part, half), cs] + decoded(last_in.at[0, front, cs], last_scale_in.at[0, :, cs])
+                put_last(ahead, 1, 0, cs)
+                behind = sums[pl.ds(2 * part + half, half), cs] + decoded(
+                    last_in.at[0, back, cs], last_scale_in.at[1, :, cs]
+                )
+                put_last(behind, 2, 1, cs)
+
+            each_tile(q, body)
+            start(last(q, 1, 0))
+            start(last(q, 2, 1))
 
         exchanged(*stat(1, 2)).wait_recv()
         spread_first[core] = added(stats.at[1, 2])
         spread_push.start()
-        for q in range(3):
-            arrived(last_both(q, 0))
-
-            def body(cs):
-                ahead = jnp.concatenate(
-                    [
-                        sums[pl.ds(part, half), cs] + decoded(last_in.at[0, front, cs], last_scale_in.at[0, :, cs]),
-                        sums[pl.ds(part + half, half), cs],
-                    ],
-                    axis=0,
-                )
-                encoded(ahead, last_out.at[1, :, cs], last_scale.at[1, :, cs])
-                behind = jnp.concatenate(
-                    [
-                        sums[pl.ds(2 * part, half), cs],
-                        sums[pl.ds(2 * part + half, half), cs]
-                        + decoded(last_in.at[0, back, cs], last_scale_in.at[1, :, cs]),
-                    ],
-                    axis=0,
-                )
-                encoded(behind, last_out.at[2, :, cs], last_scale.at[2, :, cs])
-
-            each_tile(q, body)
-            start(last(q, 1))
-            start(last(q, 2))
-
         spread_push.wait_recv()
-        grand_count = added(stats.at[0, 2])[2, 0, 0]
+        grand_count = added(stats.at[0, 2])[0, 0, width]
         row_block = me[0] * 16 + me[1] * 4 + me[2]
         in_half = lax.rem(row_block, half_blocks)
         lane_block = cs_of(in_half * block // LANE)
@@ -597,11 +605,14 @@
             arrived(last_both(q, 1))
 
             def body(cs):
-                cross = (
-                    sums[pl.ds(3 * part, part), cs]
-                    + decoded(last_in.at[1, :, cs], last_scale_in.at[2, :, cs])
-                    + decoded(last_in.at[2, :, cs], last_scale_in.at[3, :, cs])
-                )
+                halves = []
+                for way, lines in ((0, front), (1, back)):
+                    halves.append(
+                        sums[pl.ds(3 * part + way * half, half), cs]
+                        + decoded(last_in.at[1, lines, cs], last_scale_in.at[2 + way, :, cs])
+                        + decoded(last_in.at[2, lines, cs], last_scale_in.at[4 + way, :, cs])
+                    )
+                cross = jnp.concatenate(halves, axis=0)
                 columns_var = spread_first[core, 1, :, cs] / grand_count + 0.1
                 out_ref[pl.ds(0, block), cs] = cross / grand_count * lax.rsqrt(rows_var * columns_var)
 
@@ -609,9 +620,8 @@
 
         out_ref[pl.ds(block, 2), :] = grand[0:2, :]
 
-        for q in range(3):
-            for copies in (near_all(q), mid_all(q), last_all(q)):
-                gone(copies)
+        for copies in (near_all(), mid_all(), last_all()):
+            gone(copies)
         for copy in (main_push, late_push, spread_push):
             copy.wait_send()
         for d in range(3):
@@ -651,19 +661,19 @@
             vmem((4, 1, width), f32), vmem((8, 1, width), f32),
             vmem((8, 1, width), f32), vmem((8, 1, width), f32),
             vmem((3, 1, width), f32), vmem((4, 1, width), f32),
-            vmem((3, 1, width), f32), vmem((4, 1, width), f32),
-            vmem((2, 8, width), f32), vmem((2, 8, width), f32),
-            vmem((3, 4, 3, 1, width), f32),
-            vmem((2, 3, 4, 3, 1, width), f32),
-            vmem((2, 3, 1, width), f32),
+            vmem((6, 1, width), f32), vmem((6, 1, width), f32),
+            vmem((2, 8, width), f32), vmem((2, 8, width), f32), vmem((tokens // 4, LANE), bf16),
+            vmem((3, 4, 2, 1, width + LANE), f32),
+            vmem((2, 3, 4, 2, 1, width + LANE), f32),
+            vmem((2, 2, 1, width + LANE), f32),
             vmem((8, width), f32),
             vmem((LANE, LANE), f32),
             dma((2, 4)), dma((3,)), dma((3,)),
             dma((3,)), dma((3,)), dma((2, 3)), dma((2, 3)),
-            dma((3,)), dma((3, 4)), dma((3,)), dma((3, 4)),
-            dma((3,)), dma((3, 4)), dma((3,)), dma((3, 4)),
-            dma((3,)), dma((3, 2)), dma((3,)), dma((3, 2)),
-            dma((3,)), dma((3, 2)), dma((3,)), dma((3, 2)),
+            dma((1,)), dma((1, 4)), dma((1,)), dma((1, 4)),
+            dma((1,)), dma((3, 4)), dma((1,)), dma((3, 4)),
+            dma((1,)), dma((3, 2)), dma((1,)), dma((3, 2)),
+            dma((1,)), dma((3, 2)), dma((1,)), dma((3, 2)),
         ],
         compiler_params=pltpu.CompilerParams(
             collective_id=0, has_side_effects=True, vmem_limit_bytes=67_043_328
@@ -673,7 +683,18 @@
         ),
         name="whole",
     )(window_counts, first_acts, second_acts)
-    return out[:block], out[block : block + 2]
+
+    def cut(out_ref, whitened_ref, means_ref):
+        whitened_ref[...] = out_ref[:block]
+        means_ref[...] = out_ref[block : block + 2]
+
+    return tuple(
+        pl.pallas_call(
+            cut,
+            out_shape=(jax.ShapeDtypeStruct((block, width), f32), jax.ShapeDtypeStruct((2, width), f32)),
+            name="cut",
+        )(out)
+    )
 
 
 def solution(mesh):

time: 104 us -> 98.9 us (0.951)
  local copies, waits for them, and re-layouts: 3.32 us -> 0 us
  Pallas kernels: 99.3 us -> 98.1 us
    slice x2 -> x0, local copies, waits for them, and re-layouts: 3.32 us -> none  [local(): return (out[:block], out[block:block + 2])]
    pallas_call x1, Pallas kernels: 99.3 us -> 96.2 us  [local(): pl.pallas_call(functools.partial(kernel, widths_of(width)), out_shape=jax...]
    pallas_call x0 -> x1, Pallas kernels: none -> 1.9 us  [local(): pl.pallas_call(cut, out_shape=(jax.ShapeDtypeStruct((block, width), f32),...]
where the time goes in v6:
time: 98.9 us; the launch traced here: 98.8 us
  Pallas kernels  98.1 us (99%)
    pallas_call x1, Pallas kernels, local(): pl.pallas_call(functools.partial(kernel, widths_of(width)), out_shape=jax...  96.2 us

profile of v6, /device:TPU:0, one launch (start us, length us, event | category | flops | bytes accessed | tf_op | source)
XLA Modules:
  0.0 98.8 jit_solution(2475227486675324617)
XLA Ops:
  0.6 96.2 %whole.1.out_ref = f32[72,2048]{1,0:T(8,128)} custom-call(s32[4]{0:T(128)} %counts_ref.1, bf16[1536,2048]{1,0:T(8,128)(2,1)} %first_hbm.1, bf16[1536,2048]{1,0:T(8,128)(2,1)} %second_hbm.1), custom_call_target="tpu_custom_call" | custom-call | flops 30064771072 | bytes 30000000 | tf_op jit(solution)/shard_map/whole/pallas_call | solution.py:645
  96.9 1.9 %cut.1 = (f32[64,2048]{1,0:T(8,128)}, f32[2,2048]{1,0:T(2,128)}) custom-call(f32[72,2048]{1,0:T(8,128)} %whole.1.out_ref), custom_call_target="tpu_custom_call" | custom-call | tf_op jit(solution)/shard_map/cut/pallas_call | solution.py:692

commit v7 on v6

--- a/solution.py
+++ b/solution.py
@@ -360,34 +360,33 @@
                 if q < 2:
                     multiply(q + 1, 2, distance_of(k))
                 else:
-                    multiply(0, jnp.where(k == 3, 1, 2), pick(k, DISTANCES[1:] + DISTANCES[:1]))
+                    multiply(0, jnp.where(k == 3, 1 + 2 * core, 2), pick(k, DISTANCES[1:] + DISTANCES[:1]))
                 encode_sums(q, far_out.at[k], far_scale.at[k])
             for q in range(3):
                 start(far(q, k, 0))
                 start(far(q, k, 1))
 
         def serve_near(k):
-            for way in (0, 1):
+            for turn in (0, 1):
+                way = turn + core - 2 * turn * core
+                later = 1 - way
                 n = 2 * k + way
-                if way == 0:
+                lines = pl.ds(pl.multiple_of(way * (rows // 2), rows // 2), rows // 2)
+                if turn == 0:
                     arrived(far_both(k))
                 for q in range(3):
                     if q < 2:
-                        multiply(q + 1, (1, 3)[way], distance_of(k))
-                    elif way == 0:
-                        multiply(0, 3, distance_of(k))
+                        multiply(q + 1, 1 + 2 * way, distance_of(k))
+                    elif turn == 0:
+                        multiply(0, 1 + 2 * later, distance_of(k))
                     else:
-                        multiply(0, jnp.where(k == 3, 0, 1), pick(k, DISTANCES[1:] + DISTANCES[3:]))
+                        multiply(0, jnp.where(k == 3, 0, 1 + 2 * core), pick(k, DISTANCES[1:] + DISTANCES[3:]))
                     for cs in tiles(q):
-                        p = sums[:, cs]
-                        more = decoded(far_in.at[k, (upper, lower)[way], cs], far_scale_in.at[n, :, cs])
-                        if way == 0:
-                            p = jnp.concatenate([p[: rows // 2] + more, p[rows // 2 :]], axis=0)
-                        else:
-                            p = jnp.concatenate([p[: rows // 2], p[rows // 2 :] + more], axis=0)
-                        encoded(p, near_out.at[n, :, cs], near_scale.at[n, :, cs])
+                        more = decoded(far_in.at[k, lines, cs], far_scale_in.at[n, :, cs])
+                        sums[lines, cs] += more
+                        encoded(sums[:, cs], near_out.at[n, :, cs], near_scale.at[n, :, cs])
                 for q in range(3):
-                    start(near(q, n, (1, 3)[way]))
+                    start(near(q, n, 1 + 2 * way))
 
         multiply(0, 2, DISTANCES[0])
         for q in range(3):

time: 98.9 us -> 99.2 us (level)
  no operation moved by 1% of the time
where the time goes in v7:
time: 99.2 us; the launch traced here: 98.1 us
  Pallas kernels  97.5 us (98%)
    pallas_call x1, Pallas kernels, local(): pl.pallas_call(functools.partial(kernel, widths_of(width)), out_shape=jax...  95.6 us

profile of v7, /device:TPU:0, one launch (start us, length us, event | category | flops | bytes accessed | tf_op | source)
XLA Modules:
  0.0 98.1 jit_solution(12423188282368982809)
XLA Ops:
  0.6 95.6 %whole.1.out_ref = f32[72,2048]{1,0:T(8,128)} custom-call(s32[4]{0:T(128)} %counts_ref.1, bf16[1536,2048]{1,0:T(8,128)(2,1)} %first_hbm.1, bf16[1536,2048]{1,0:T(8,128)(2,1)} %second_hbm.1), custom_call_target="tpu_custom_call" | custom-call | flops 30064771072 | bytes 30000000 | tf_op jit(solution)/shard_map/whole/pallas_call | solution.py:644
  96.2 1.9 %cut.1 = (f32[64,2048]{1,0:T(8,128)}, f32[2,2048]{1,0:T(2,128)}) custom-call(f32[72,2048]{1,0:T(8,128)} %whole.1.out_ref), custom_call_target="tpu_custom_call" | custom-call | tf_op jit(solution)/shard_map/cut/pallas_call | solution.py:691
